TPU v7x, 256 devices: a whole 4x4x8 slice. The times are simulated.
256 devices in a mesh: grid: 32 (over z, y), atom: 8 (over x, core).
Axes of the slice: x: 4, y: 4, z: 8, core: 2. Of those that a mesh axis runs over, the one named last changes fastest.
Arguments:
- weights: float32 [4194304], P(('grid', 'atom')), may hold values from 0.25 to 4
- target: float32 [4194304], P(('grid', 'atom')), may hold values from -6 to 6
- coupling: float32 [4194304], P(('grid', 'atom')), may hold values from -0.9 to 0.9
- multipole_basis: float32 [25, 4194304], P(None, ('grid', 'atom')), may hold values from -6 to 6
- rho_hist: float32 [8, 4194304], P(None, ('grid', 'atom')), may hold values from -6 to 6
- res_hist: float32 [8, 4194304], P(None, ('grid', 'atom')), may hold values from -6 to 6
- batch_atom: int32 [16384], P(('grid', 'atom')), may hold values from 0 to 4095
- owner_slot: int32 [4096], replicated, may hold values from 0 to 4095, each once
- slot_index: int32 [2], replicated, may hold values from 0 to 7
Outputs:
- density: float32 [4194304], P(('grid', 'atom'))
- moments: float32 [25, 4096], P(None, 'atom')
Inputs may be any that keep to these rules, and one draw needn't show every extreme that they name: `owner_slot`: each slot 0 to 4095 belongs to exactly one atom.
All inputs are finite; a program needn't handle non-finite values.
Results may differ from a plain program's by a relative error of at most 0.00011.
Values sent between devices are 32-bit elements; how exact they have to be, the bound alone decides.
A program may use at most 64 MiB of HBM per device.

v0:
```python
import math

import jax
import jax.numpy as jnp
import numpy as np
from jax import lax
from jax.sharding import Mesh
from jax.sharding import PartitionSpec as P

ITERS = 2
GRID_ATOM = ("grid_0", "grid_1", "atom_0", "atom_1")
ATOM = ("atom_0", "atom_1")
GRID = ("grid_0", "grid_1")


damping_table = np.array(
    [1.0 / (1 + degree) for degree in range(5) for order in range(2 * degree + 1)], dtype=np.float32
)
mixing_beta = 0.5
ridge_share = 0.1


def over_axes(value, axes):
    for axis in axes:
        value = lax.psum(value, axis)
    return value


def in_blocks(value, dim, peers):
    lengths = value.shape
    pieces = value.reshape(*lengths[:dim], peers, lengths[dim] // peers, *lengths[dim + 1 :])
    return jnp.moveaxis(pieces, dim, 0)


def sent_and_summed(value, axis, dim):
    peers = lax.axis_size(axis)
    pieces = lax.all_to_all(in_blocks(value, dim, peers), axis, 0, 0, tiled=True)
    return jnp.sum(pieces, axis=0)


def mixing_weights(intersect):
    hist_len = intersect.shape[0]
    ridge_val = ridge_share * jnp.trace(intersect) / hist_len
    shifted = intersect + ridge_val * jnp.eye(hist_len, dtype=intersect.dtype)
    factor = jnp.linalg.cholesky(shifted)
    forward = []
    for row_at in range(hist_len):
        entry_val = 1.0
        for col_at in range(row_at):
            entry_val = entry_val - factor[row_at, col_at] * forward[col_at]
        forward.append(entry_val / factor[row_at, row_at])
    backward = [None] * hist_len
    for row_at in reversed(range(hist_len)):
        entry_val = forward[row_at]
        for col_at in range(row_at + 1, hist_len):
            entry_val = entry_val - factor[col_at, row_at] * backward[col_at]
        backward[row_at] = entry_val / factor[row_at, row_at]
    solved = jnp.stack(backward)
    return solved / jnp.sum(solved)


def intersect_total(intersect_part):
    return over_axes(intersect_part, GRID_ATOM)


def moments_total(moment_part):
    owned_moms = sent_and_summed(moment_part, ATOM, 1)
    owned_moms = over_axes(owned_moms, GRID)
    all_moments = lax.all_gather(owned_moms, ATOM, axis=1, tiled=True)
    return (owned_moms, all_moments)


def local(
    weights,
    target,
    coupling,
    multipole_basis,
    rho_hist,
    res_hist,
    batch_atom,
    owner_slot,
    slot_index,
):
    hi_prec = lax.Precision.HIGHEST
    harmonics = multipole_basis.shape[0]
    points = weights.shape[0]
    batch_count = batch_atom.shape[0]
    batch_width = points // batch_count
    atom_total = owner_slot.shape[0]
    owned_count = atom_total // lax.axis_size(ATOM)
    atom_points = points * lax.axis_size(GRID) // owned_count
    moment_scale = 1.0 / math.sqrt(atom_points)
    damping = jnp.asarray(damping_table, dtype=weights.dtype)
    batch_slot = owner_slot[batch_atom]
    one_hot = (batch_slot[:, None] == jnp.arange(atom_total, dtype=jnp.int32)[None, :]).astype(
        weights.dtype
    )
    basis_blocks = multipole_basis.reshape(harmonics, batch_count, batch_width)
    intersect = None
    density = None
    owned_moms = None
    res_new = None
    previous = None
    for iteration in range(ITERS):
        fresh_start = iteration == 0
        if fresh_start:
            intersect_part = jnp.dot(res_hist * weights[None, :], res_hist.T, precision=hi_prec)
        else:
            intersect_part = jnp.dot(res_hist * weights[None, :], res_new, precision=hi_prec)
        if fresh_start:
            intersect = intersect_total(intersect_part)
        else:
            new_row = intersect_total(intersect_part)
            intersect = intersect.at[previous, :].set(new_row).at[:, previous].set(new_row)
        coeffs = mixing_weights(intersect)
        res_mix = jnp.dot(coeffs, res_hist, precision=hi_prec)
        fields = res_mix[None, :]
        leading = fields.shape[0]
        weighted = (fields * weights[None, :]).reshape(leading, 1, batch_count, batch_width)
        per_batch = jnp.sum(weighted * basis_blocks[None], axis=3)
        summed = jnp.dot(
            per_batch.reshape(leading * harmonics, batch_count), one_hot, precision=hi_prec
        )
        owned_moms, all_moments = moments_total(
            (summed.reshape(leading, harmonics, atom_total) * moment_scale)[0]
        )
        rho_mix = jnp.dot(coeffs, rho_hist, precision=hi_prec)
        at_batch = jnp.dot(all_moments * damping[:, None], one_hot.T, precision=hi_prec)
        density = rho_mix + mixing_beta * (
            res_mix - jnp.sum(at_batch[:, :, None] * basis_blocks, axis=0).reshape(points)
        )
        res_new = target + coupling * jnp.tanh(density) - density
        previous = slot_index[iteration]
        rho_hist = rho_hist.at[previous].set(density)
        res_hist = res_hist.at[previous].set(res_new)
    return (density, owned_moms)


def solution(mesh):
    torus = Mesh(mesh.devices.reshape(8, 4, 4, 2), ("grid_0", "grid_1", "atom_0", "atom_1"))
    placed = (
        P(GRID_ATOM),
        P(GRID_ATOM),
        P(GRID_ATOM),
        P(None, GRID_ATOM),
        P(None, GRID_ATOM),
        P(None, GRID_ATOM),
        P(GRID_ATOM),
        P(),
        P(),
    )
    return jax.shard_map(
        local, mesh=torus, in_specs=placed, out_specs=(P(GRID_ATOM), P(None, ATOM)), check_vma=False
    )
```

profile of v0, /device:TPU:1, one launch (start us, length us, event | category | flops | bytes accessed | tf_op | source)
XLA Modules:
  0.0 349.3 jit_solution(12972554845660243623)
XLA Ops:
  2.9 1.2 fusion.4
  4.1 17.3 %psum.84 = f32[8,8]{0,1:T(8,128)S(1)} all-reduce(f32[8,8]{0,1:T(8,128)S(1)} %fusion.4), channel_id=1, replica_groups=mesh['grid_0'=8,'grid_1'=4,'atom_0'=4,'atom_1'=2] {'grid_0'}, use_global_device_ids=true, to_apply=%region_0.0 | all-reduce | flops 64 | bytes 512 | tf_op jit(solution)/shard_map/psum | solution.py:25
  21.4 8.7 %psum.85 = f32[8,8]{0,1:T(8,128)S(1)} all-reduce(f32[8,8]{0,1:T(8,128)S(1)} %psum.84), channel_id=1, replica_groups=mesh['grid_0'=8,'grid_1'=4,'atom_0'=4,'atom_1'=2] {'grid_1'}, use_global_device_ids=true, to_apply=%region_1.0 | all-reduce | flops 64 | bytes 512 | tf_op jit(solution)/shard_map/psum | solution.py:25
  30.2 8.5 %psum.86 = f32[8,8]{0,1:T(8,128)S(1)} all-reduce(f32[8,8]{0,1:T(8,128)S(1)} %psum.85), channel_id=1, replica_groups=mesh['grid_0'=8,'grid_1'=4,'atom_0'=4,'atom_1'=2] {'atom_0'}, use_global_device_ids=true, to_apply=%region_2.0 | all-reduce | flops 64 | bytes 512 | tf_op jit(solution)/shard_map/psum | solution.py:25
  38.6 10.4 %psum.87 = f32[8,8]{0,1:T(8,128)S(1)} all-reduce(f32[8,8]{0,1:T(8,128)S(1)} %psum.86), channel_id=1, replica_groups=mesh['grid_0'=8,'grid_1'=4,'atom_0'=4,'atom_1'=2] {'atom_1'}, use_global_device_ids=true, to_apply=%region_3.0 | all-reduce | flops 64 | bytes 512 | tf_op jit(solution)/shard_map/psum | solution.py:25
  101.1 1.3 copy-done.2
  105.4 4.4 %all-to-all-start = ((f32[8,25,512]{2,1,0:T(8,128)}), f32[8,25,512]{2,1,0:T(8,128)}, u32[]{:S(2)}, u32[]{:S(2)}) async-start(f32[8,25,512]{2,1,0:T(8,128)} %bitcast.166), calls=%async_computation | async-start | bytes 1048576 | tf_op jit(solution)/shard_map/all_to_all | solution.py:37
  111.2 8.1 %all-to-all-done = f32[8,25,512]{2,1,0:T(8,128)} async-done(((f32[8,25,512]{2,1,0:T(8,128)}), f32[8,25,512]{2,1,0:T(8,128)}, u32[]{:S(2)}, u32[]{:S(2)}) %all-to-all-start) | async-done | bytes 409632 | tf_op jit(solution)/shard_map/all_to_all | solution.py:37
  120.4 20.6 %psum.88 = f32[25,512]{1,0:T(8,128)S(1)} all-reduce(f32[25,512]{1,0:T(8,128)S(1)} %reduce_sum.129), channel_id=1, replica_groups=mesh['grid_0'=8,'grid_1'=4,'atom_0'=4,'atom_1'=2] {'grid_0'}, use_global_device_ids=true, to_apply=%region_10.12 | all-reduce | flops 12800 | bytes 102400 | tf_op jit(solution)/shard_map/psum | solution.py:25
  141.0 11.3 %psum.89 = f32[25,512]{1,0:T(8,128)S(1)} all-reduce(f32[25,512]{1,0:T(8,128)S(1)} %psum.88), channel_id=1, replica_groups=mesh['grid_0'=8,'grid_1'=4,'atom_0'=4,'atom_1'=2] {'grid_1'}, use_global_device_ids=true, to_apply=%region_11.13 | all-reduce | flops 12800 | bytes 102400 | tf_op jit(solution)/shard_map/psum | solution.py:25
  152.4 24.2 %all_gather.6 = f32[25,4096]{1,0:T(8,128)S(1)} all-gather(f32[25,512]{1,0:T(8,128)S(1)} %psum.89), channel_id=1, replica_groups=mesh['grid_0'=8,'grid_1'=4,'atom_0'=4,'atom_1'=2] {'atom_0','atom_1'}, dimensions={1}, use_global_device_ids=true | all-gather | bytes 460800 | tf_op jit(solution)/shard_map/all_gather | solution.py:69
  177.8 1.2 copy.29
  181.2 1.2 convolution_bitcast_fusion
  182.5 12.3 %psum.90 = f32[8]{0:T(128)S(1)} all-reduce(f32[8]{0:T(128)S(1)} %convolution_bitcast_fusion), channel_id=1, replica_groups=mesh['grid_0'=8,'grid_1'=4,'atom_0'=4,'atom_1'=2] {'grid_0'}, use_global_device_ids=true, to_apply=%region_13.15 | all-reduce | flops 8 | bytes 64 | tf_op jit(solution)/shard_map/psum | solution.py:25
  194.8 7.7 %psum.91 = f32[8]{0:T(128)S(1)} all-reduce(f32[8]{0:T(128)S(1)} %psum.90), channel_id=1, replica_groups=mesh['grid_0'=8,'grid_1'=4,'atom_0'=4,'atom_1'=2] {'grid_1'}, use_global_device_ids=true, to_apply=%region_14.16 | all-reduce | flops 8 | bytes 64 | tf_op jit(solution)/shard_map/psum | solution.py:25
  202.5 6.8 %psum.92 = f32[8]{0:T(128)S(1)} all-reduce(f32[8]{0:T(128)S(1)} %psum.91), channel_id=1, replica_groups=mesh['grid_0'=8,'grid_1'=4,'atom_0'=4,'atom_1'=2] {'atom_0'}, use_global_device_ids=true, to_apply=%region_15.17 | all-reduce | flops 8 | bytes 64 | tf_op jit(solution)/shard_map/psum | solution.py:25
  210.0 10.0 %psum.93 = f32[8]{0:T(128)S(1)} all-reduce(f32[8]{0:T(128)S(1)} %psum.92), channel_id=1, replica_groups=mesh['grid_0'=8,'grid_1'=4,'atom_0'=4,'atom_1'=2] {'atom_1'}, use_global_device_ids=true, to_apply=%region_16.18 | all-reduce | flops 8 | bytes 64 | tf_op jit(solution)/shard_map/psum | solution.py:25
  272.7 1.7 fusion.1
  276.4 3.7 %all-to-all-start.1 = ((f32[8,25,512]{2,1,0:T(8,128)}), f32[8,25,512]{2,1,0:T(8,128)S(1)}, u32[]{:S(2)}, u32[]{:S(2)}) async-start(f32[8,25,512]{2,1,0:T(8,128)} %bitcast.156), calls=%async_computation.1 | async-start | bytes 1048576 | tf_op jit(solution)/shard_map/all_to_all | solution.py:37
  281.1 8.3 %all-to-all-done.1 = f32[8,25,512]{2,1,0:T(8,128)S(1)} async-done(((f32[8,25,512]{2,1,0:T(8,128)}), f32[8,25,512]{2,1,0:T(8,128)S(1)}, u32[]{:S(2)}, u32[]{:S(2)}) %all-to-all-start.1) | async-done | bytes 409632 | tf_op jit(solution)/shard_map/all_to_all | solution.py:37
  289.5 20.7 %psum.94 = f32[25,512]{1,0:T(8,128)S(1)} all-reduce(f32[25,512]{1,0:T(8,128)S(1)} %reduce_sum.140), channel_id=1, replica_groups=mesh['grid_0'=8,'grid_1'=4,'atom_0'=4,'atom_1'=2] {'grid_0'}, use_global_device_ids=true, to_apply=%region_21.23 | all-reduce | flops 12800 | bytes 102400 | tf_op jit(solution)/shard_map/psum | solution.py:25
  310.2 11.3 %psum.95 = f32[25,512]{1,0:T(8,128)S(1)} all-reduce(f32[25,512]{1,0:T(8,128)S(1)} %psum.94), channel_id=1, replica_groups=mesh['grid_0'=8,'grid_1'=4,'atom_0'=4,'atom_1'=2] {'grid_1'}, use_global_device_ids=true, to_apply=%region_22.24 | all-reduce | flops 12800 | bytes 102400 | tf_op jit(solution)/shard_map/psum | solution.py:25
  321.6 24.2 %all_gather.7 = f32[25,4096]{1,0:T(8,128)S(1)} all-gather(f32[25,512]{1,0:T(8,128)S(1)} %psum.95), channel_id=1, replica_groups=mesh['grid_0'=8,'grid_1'=4,'atom_0'=4,'atom_1'=2] {'atom_0','atom_1'}, dimensions={1}, use_global_device_ids=true | all-gather | bytes 460800 | tf_op jit(solution)/shard_map/all_gather | solution.py:69
  347.0 1.2 copy.31
  (88 shorter events, 29.1 us)
Async XLA Ops:
  0.6 102.0 %copy-start = (s32[4096]{0:T(1024)S(1)}, s32[4096]{0:T(1024)}, u32[]{:S(2)}) copy-start(s32[4096]{0:T(1024)} %param.26) | copy-start | bytes 49156
  0.6 2.3 copy-start.3
  0.7 99.7 %copy-start.1 = (f32[25,16384]{1,0:T(8,128)S(1)}, f32[25,16384]{1,0:T(8,128)}, u32[]{:S(2)}) copy-start(f32[25,16384]{1,0:T(8,128)} %param.22) | copy-start | bytes 4915204
  100.3 0.7 copy-start.10
  101.0 1.4 copy-start.2
  103.5 6.3 %copy-start.8 = (s32[2]{0:T(128)S(1)}, s32[2]{0:T(128)}, u32[]{:S(2)}) copy-start(s32[2]{0:T(128)} %param.27) | copy-start | bytes 28
  103.5 6.5 %copy-start.9 = (s32[2]{0:T(128)S(1)}, s32[2]{0:T(128)}, u32[]{:S(2)}) copy-start(s32[2]{0:T(128)} %constant.135.clone.1) | copy-start | bytes 28
  104.4 72.2 %copy-start.7 = (f32[25]{0:T(128)S(1)}, f32[25]{0:T(128)}, u32[]{:S(2)}) copy-start(f32[25]{0:T(128)} %constant.143.clone) | copy-start | bytes 304
  105.4 13.8 %all-to-all-start = ((f32[8,25,512]{2,1,0:T(8,128)}), f32[8,25,512]{2,1,0:T(8,128)}, u32[]{:S(2)}, u32[]{:S(2)}) async-start(f32[8,25,512]{2,1,0:T(8,128)} %bitcast.166), calls=%async_computation | async-start | bytes 1048576 | tf_op jit(solution)/shard_map/all_to_all | solution.py:37
  179.0 0.8 copy-start.5
  179.0 0.9 copy-start.6
  276.4 13.1 %all-to-all-start.1 = ((f32[8,25,512]{2,1,0:T(8,128)}), f32[8,25,512]{2,1,0:T(8,128)S(1)}, u32[]{:S(2)}, u32[]{:S(2)}) async-start(f32[8,25,512]{2,1,0:T(8,128)} %bitcast.156), calls=%async_computation.1 | async-start | bytes 1048576 | tf_op jit(solution)/shard_map/all_to_all | solution.py:37
  321.5 25.4 %copy-start.4 = (f32[25,512]{1,0:T(8,128)}, f32[25,512]{1,0:T(8,128)S(1)}, u32[]{:S(2)}) copy-start(f32[25,512]{1,0:T(8,128)S(1)} %psum.95) | copy-start | bytes 153604
where the time goes:
time: 351 us; the launch traced here: 349 us
  blocking collectives  194 us (55%)
  between operations  93.7 us (27%)
  waiting for transfers between devices  16.4 us (5%)
  local copies, waits for them, and re-layouts  16.2 us (5%)
  other arithmetic  13.6 us (4%)
  starting transfers between devices  8.09 us (2%)
  matrix products  7.31 us (2%)
    psum x12, blocking collectives, over_axes(): value = lax.psum(value, axis)  146 us
    all_gather x2, blocking collectives, moments_total(): all_moments = lax.all_gather(owned_moms, ATOM, axis=1, tiled=True)  48.4 us
    all_to_all x2, waiting for transfers between devices, sent_and_summed(): lax.all_to_all(in_blocks(value, dim, peers), axis, 0, 0, tiled=True)  16.4 us
    unnamed x31, local copies, waits for them, and re-layouts  8.14 us
    all_to_all x2, starting transfers between devices, sent_and_summed(): lax.all_to_all(in_blocks(value, dim, peers), axis, 0, 0, tiled=True)  8.09 us
  transfers between devices with their start and end apart: 2, of which 2 were waited for; matrix products, arithmetic and copies ran while one was open for 1% of the time, Pallas kernels for 0%

commit v1 on v0

v1 whole, which is shorter than its diff:
```python
import jax
import jax.numpy as jnp
from jax import lax
from jax.experimental import pallas as pl
from jax.experimental.pallas import tpu as pltpu
from jax.sharding import Mesh
from jax.sharding import PartitionSpec as P

AXES = ("z", "y", "x", "c")
SIZES = {"z": 8, "y": 4, "x": 4, "c": 2}
HIST = 8
LANES = 128
MESH = pl.DeviceIdType.MESH
F32 = jnp.float32
MIX_BETA = 0.5
RIDGE_SHARE = 0.1
GROUP = 16
ROWS = 13
INT0_A, INT0_B, META_A, META_B, PB0_A, PB0_B, INT1_A, INT1_B, PB1_A, PB1_B, MOM_B, MOM_Z = range(12)
EXCHANGES = 12
LD_RES, LD_W, LD_ATOM, LD_OWNER, LD_BASIS, LD_RHO, LD_TARGET, LD_COUPLING, ST_DEN, ST_MOM = range(10)
LOCALS = 10


def iota(shape, dim):
    return lax.broadcasted_iota(jnp.int32, shape, dim)


def sublane_total(x):
    x = x + pltpu.roll(x, 4, 0)
    x = x + pltpu.roll(x, 2, 0)
    return x + pltpu.roll(x, 1, 0)


def mixing_weights(entry):
    matrix = [[entry[i][j] for j in range(i + 1)] for i in range(HIST)]
    trace = matrix[0][0]
    for i in range(1, HIST):
        trace = trace + matrix[i][i]
    ridge = trace * (RIDGE_SHARE / HIST)
    for i in range(HIST):
        matrix[i][i] = matrix[i][i] + ridge
    forward = [jnp.ones((8, LANES), F32) for _ in range(HIST)]
    pivot = [None] * HIST
    lower = [[None] * HIST for _ in range(HIST)]
    for j in range(HIST):
        pivot[j] = 1.0 / matrix[j][j]
        for i in range(j + 1, HIST):
            ratio = matrix[i][j] * pivot[j]
            for k in range(j + 1, i + 1):
                matrix[i][k] = matrix[i][k] - ratio * matrix[k][j]
            forward[i] = forward[i] - ratio * forward[j]
            lower[i][j] = ratio
    solved = [None] * HIST
    for i in reversed(range(HIST)):
        value = forward[i] * pivot[i]
        for k in range(i + 1, HIST):
            value = value - lower[k][i] * solved[k]
        solved[i] = value
    total = solved[0]
    for i in range(1, HIST):
        total = total + solved[i]
    scale = 1.0 / total
    return [value * scale for value in solved]


def history_column(values):
    sub = iota((8, LANES), 0)
    column = jnp.zeros((8, LANES), F32)
    for i in range(HIST):
        column = jnp.where(sub == i, values[i], column)
    return column


def three_parts(x):
    high = x.astype(jnp.bfloat16)
    rest = x - high.astype(F32)
    middle = rest.astype(jnp.bfloat16)
    low = (rest - middle.astype(F32)).astype(jnp.bfloat16)
    return jnp.concatenate([high, middle, low], axis=0)


def body(
    w_h, t_h, cpl_h, basis_h, rho_h, res_h, atom_h, owner_h, slot_index,
    den_h, mom_h,
    w, t, cpl, basis, rho, res, atom, owner, den, rnew, mom,
    entries, same_atom, same_slot,
    int0_a, int0_b, int1_a, int1_b, meta_a, meta_b,
    pb0_a, pb0_b, pb1_a, pb1_b, mom_b, mom_z, send0, send1, send2,
    local_sem, send_sem, recv_sem,
):
    me = {name: lax.axis_index(name) for name in AXES}
    own_a = me["y"] * 4 + me["x"]
    own_b = me["c"] * 8 + me["z"]
    blocks = w.shape[0]

    loads = {}
    for key, src, dst in (
        (LD_RES, res_h, res), (LD_W, w_h, w), (LD_ATOM, atom_h, atom), (LD_OWNER, owner_h, owner),
        (LD_BASIS, basis_h, basis), (LD_RHO, rho_h, rho), (LD_TARGET, t_h, t), (LD_COUPLING, cpl_h, cpl),
    ):
        loads[key] = pltpu.make_async_copy(src, dst, local_sem.at[key])
        loads[key].start()

    peers_a = []
    for dy in range(4):
        for dx in range(4):
            if dy or dx:
                peers_a.append({"y": lax.rem(me["y"] + dy, 4), "x": lax.rem(me["x"] + dx, 4)})
    peers_b = []
    for dc in range(2):
        for dz in range(8):
            if dc or dz:
                peers_b.append({"z": lax.rem(me["z"] + dz, 8), "c": lax.rem(me["c"] + dc, 2)})

    barrier = pltpu.get_barrier_semaphore()
    for peer in peers_a + peers_b:
        pl.semaphore_signal(barrier, inc=1, device_id=peer, device_id_type=MESH)

    def send(src, dst, key, peer):
        pltpu.make_async_remote_copy(
            src_ref=src, dst_ref=dst, send_sem=send_sem.at[key], recv_sem=recv_sem.at[key],
            device_id=peer, device_id_type=MESH,
        ).start()

    def gather(buf, own, key, peers):
        for peer in peers:
            send(buf.at[own], buf.at[own], key, peer)

    def arrived(buf, key, count):
        view = buf.at[pl.ds(0, count)]
        pltpu.make_async_copy(view, view, recv_sem.at[key]).wait()

    def sent(buf, key, count):
        view = buf.at[pl.ds(0, count)]
        pltpu.make_async_copy(view, view, send_sem.at[key]).wait()

    sub = iota((8, LANES), 0)
    lane = iota((8, LANES), 1)

    loads[LD_RES].wait()
    loads[LD_W].wait()

    def products(q, accs):
        accs = list(accs)
        for u in range(8):
            off = pl.multiple_of((q * 8 + u) * LANES, LANES)
            r = res[:, pl.ds(off, LANES)]
            rw = r * jnp.broadcast_to(w[pl.ds(q * 8 + u, 1), :], (8, LANES))
            accs[0] = accs[0] + rw * r
            for s in range(1, 5):
                accs[s] = accs[s] + rw * pltpu.roll(r, s, 0)
        return tuple(accs)

    zero = jnp.zeros((8, LANES), F32)
    accs = lax.fori_loop(0, blocks // 8, products, (zero,) * 5)
    placed = zero
    for s in range(5):
        total = jnp.sum(accs[s], axis=1, keepdims=True)
        placed = jnp.where(lane == 8 * s + sub, total, placed)
    int0_a[own_a] = sublane_total(placed)[0:1, :]

    pl.semaphore_wait(barrier, len(peers_a) + len(peers_b))
    gather(int0_a, own_a, INT0_A, peers_a)

    loads[LD_ATOM].wait()
    loads[LD_OWNER].wait()
    batches = 64
    wide_sub = iota((batches, LANES), 0)
    wide_lane = iota((batches, LANES), 1)
    atom_row = atom[0:1, :].astype(F32)
    atom_col = jnp.sum(
        jnp.where(wide_lane == wide_sub, jnp.broadcast_to(atom_row, (batches, LANES)), 0.0), axis=1, keepdims=True
    )

    def look_up(j, found):
        owners = jnp.broadcast_to(owner[pl.ds(j, 1), :].astype(F32), (batches, LANES))
        number = (wide_lane + j * LANES).astype(F32)
        return found + jnp.where(number == atom_col, owners, 0.0)

    found = lax.fori_loop(0, owner.shape[0], look_up, jnp.zeros((batches, LANES), F32))
    slot_col = jnp.sum(found, axis=1, keepdims=True)
    slot_wide = jnp.sum(
        jnp.where((wide_lane == wide_sub) | (wide_lane == wide_sub + batches), slot_col, 0.0), axis=0, keepdims=True
    )
    atom_wide = jnp.sum(
        jnp.where((wide_lane == wide_sub) | (wide_lane == wide_sub + batches), atom_col, 0.0), axis=0, keepdims=True
    )
    meta = jnp.concatenate([atom_wide, slot_wide], axis=0).astype(jnp.int32)
    meta_a[own_a] = meta
    meta_b[own_b] = meta
    gather(meta_a, own_a, META_A, peers_a)
    gather(meta_b, own_b, META_B, peers_b)

    def group_sum(buf, own, key):
        arrived(buf, key, GROUP - 1)
        total = buf[0]
        for i in range(1, GROUP):
            total = total + buf[i]
        return total

    int0_b[own_b] = group_sum(int0_a, own_a, INT0_A)
    gather(int0_b, own_b, INT0_B, peers_b)

    arrived(meta_a, META_A, GROUP - 1)
    arrived(meta_b, META_B, GROUP - 1)
    half = iota((1, LANES), 1) < batches
    atoms_b = [
        jnp.where(half, meta_b[2 * q, 0:1, :], meta_b[2 * q + 1, 0:1, :]).astype(F32) for q in range(GROUP // 2)
    ]
    slot_base = me["x"] * (GROUP * batches)

    def relate(s, nothing):
        both = meta_a[s].astype(F32)
        own_lane = wide_lane == wide_sub
        atoms_a = jnp.sum(jnp.where(own_lane, jnp.broadcast_to(both[0:1], (batches, LANES)), 0.0), axis=1, keepdims=True)
        slots_a = jnp.sum(jnp.where(own_lane, jnp.broadcast_to(both[1:2], (batches, LANES)), 0.0), axis=1, keepdims=True)
        at = pl.ds(pl.multiple_of(s * batches, batches), batches)
        for q in range(GROUP // 2):
            cols = pl.ds(q * LANES, LANES)
            same_atom[at, cols] = jnp.where(atoms_a == atoms_b[q], 1.0, 0.0).astype(jnp.bfloat16)
            number = (iota((1, LANES), 1) + (slot_base + q * LANES)).astype(F32)
            same_slot[at, cols] = jnp.where(slots_a == number, 1.0, 0.0).astype(jnp.bfloat16)
        return nothing

    lax.fori_loop(0, GROUP, relate, 0)

    def entry_values(row, count):
        rows = iota((count, LANES), 0)
        lanes = iota((count, LANES), 1)
        total = jnp.sum(jnp.where(rows == lanes, jnp.broadcast_to(row, (count, LANES)), 0.0), axis=1, keepdims=True)
        return jnp.broadcast_to(total, (count, LANES))

    def splat(base, i):
        return jnp.broadcast_to(entries[pl.ds(base + i, 1), :], (8, LANES))

    def batch_moments(column):
        def four(q, carry):
            k01, k2, k3 = carry
            for u in range(4):
                b = q * 4 + u
                offs, field = [], []
                for h in range(2):
                    j = q * 8 + 2 * u + h
                    off = pl.ds(pl.multiple_of(j * LANES, LANES), LANES)
                    mixed = sublane_total(column * res[:, off])
                    field.append(mixed * jnp.broadcast_to(w[pl.ds(j, 1), :], (8, LANES)))
                    offs.append(off)
                parts = []
                for kt in range(3):
                    rows = pl.ds(kt * 8, 8)
                    product = basis[rows, offs[0]] * field[0] + basis[rows, offs[1]] * field[1]
                    parts.append(jnp.sum(product, axis=1, keepdims=True))
                last = basis[24:25, offs[0]] * field[0][0:1] + basis[24:25, offs[1]] * field[1][0:1]
                last = jnp.sum(last, axis=1, keepdims=True)
                k01 = jnp.where(lane == b, parts[0], k01)
                k01 = jnp.where(lane == b + batches, parts[1], k01)
                k2 = jnp.where(lane == b + jnp.where(sub >= 4, batches, 0), parts[2], k2)
                k3 = jnp.where(lane[0:1] == b, last, k3)
            return k01, k2, k3

        return lax.fori_loop(0, batches // 4, four, (zero, zero, zero[0:1]))

    def put_moments(buf, at, k01, k2, k3):
        buf[at, 0:8] = k01
        buf[at, 8:12] = (k2 + pltpu.roll(k2, 4, 0))[0:4]
        buf[at, 12:13] = k3

    def left_sides(buf):
        is_low = iota((ROWS, LANES), 1) < batches
        lows, highs = [], []
        for q in range(GROUP // 2):
            first, second = buf[2 * q], buf[2 * q + 1]
            lows.append(jnp.where(is_low, first, pltpu.roll(second, batches, 1)))
            highs.append(jnp.where(is_low, pltpu.roll(first, batches, 1), second))
        pad = jnp.zeros((16 - ROWS, GROUP * batches), F32)
        low = jnp.concatenate(lows, axis=1)
        high = jnp.concatenate(highs, axis=1)
        return three_parts(jnp.concatenate([low, pad, high, pad], axis=0))

    def contributions(parts, matrix, out):
        result = jnp.dot(parts, matrix[...], preferred_element_type=F32)
        result = result[0:32] + result[32:64] + result[64:96]
        is_low = iota((ROWS, LANES), 1) < batches
        for q in range(GROUP // 2):
            cols = slice(q * LANES, (q + 1) * LANES)
            low, high = result[0:ROWS, cols], result[16:16 + ROWS, cols]
            out[2 * q] = jnp.where(is_low, low, pltpu.roll(high, batches, 1))
            out[2 * q + 1] = jnp.where(is_low, pltpu.roll(low, batches, 1), high)

    def scatter(out, buf, key):
        buf[own_b] = out[own_b]
        for peer in peers_b:
            send(out.at[peer.get("c") * 8 + peer.get("z")], buf.at[own_b], key, peer)

    def packed_scale(rows):
        r, c = iota((rows, LANES), 0), iota((rows, LANES), 1)
        high = c >= batches
        k = jnp.where(r < 8, jnp.where(high, r + 8, r), jnp.where(high, r + 12, r + 8))
        k = jnp.where(r == 12, 24, k)
        degree = (
            jnp.where(k >= 1, 1, 0) + jnp.where(k >= 4, 1, 0) + jnp.where(k >= 9, 1, 0) + jnp.where(k >= 16, 1, 0)
        )
        return 1.0 / (1.0 + degree.astype(F32))

    moment_scale = 1.0 / 32.0

    def mixed_density(total, column, final):
        total = total * (packed_scale(ROWS) * (MIX_BETA * moment_scale))
        first = total[0:8]
        rest = jnp.concatenate([total[8:13], jnp.zeros((3, LANES), F32)], axis=0)
        second = jnp.where(sub < 4, rest, pltpu.roll(pltpu.roll(rest, 4, 0), batches, 1))
        last = jnp.broadcast_to(rest[4:5], (8, LANES))

        def eight(q, carry):
            first, second, last = carry
            dense = zero
            for u in range(4):
                cols = (
                    jnp.broadcast_to(first[:, u:u + 1], (8, LANES)),
                    jnp.broadcast_to(first[:, batches + u:batches + u + 1], (8, LANES)),
                    jnp.broadcast_to(second[:, u:u + 1], (8, LANES)),
                )
                col_last = jnp.broadcast_to(last[:, u:u + 1], (8, LANES))
                for h in range(2):
                    r = 2 * u + h
                    off = pl.ds(pl.multiple_of((q * 8 + r) * LANES, LANES), LANES)
                    y = column * (rho[:, off] + MIX_BETA * res[:, off])
                    for kt in range(3):
                        y = y - cols[kt] * basis[kt * 8:kt * 8 + 8, off]
                    y = sublane_total(y) - col_last * jnp.broadcast_to(basis[24:25, off], (8, LANES))
                    dense = jnp.where(sub == r, y, dense)
            at = pl.ds(pl.multiple_of(q * 8, 8), 8)
            den[at, :] = dense
            if not final:
                rnew[at, :] = t[at, :] + cpl[at, :] * jnp.tanh(dense) - dense
            return tuple(pltpu.roll(x, LANES - 4, 1) for x in (first, second, last))

        lax.fori_loop(0, blocks // 8, eight, (first, second, last))

    row = group_sum(int0_b, own_b, INT0_B)
    entries[0:40, :] = entry_values(row, 40)

    def pair(i, j):
        s = (i - j) % 8
        return splat(0, 8 * s + i) if s <= 4 else splat(0, 8 * ((j - i) % 8) + j)

    column0 = history_column(mixing_weights([[pair(i, j) for j in range(i + 1)] for i in range(HIST)]))
    loads[LD_BASIS].wait()
    put_moments(pb0_a, own_a, *batch_moments(column0))
    gather(pb0_a, own_a, PB0_A, peers_a)
    arrived(pb0_a, PB0_A, GROUP - 1)
    contributions(left_sides(pb0_a), same_atom, send0)
    scatter(send0, pb0_b, PB0_B)
    loads[LD_RHO].wait()
    loads[LD_TARGET].wait()
    loads[LD_COUPLING].wait()
    mixed_density(group_sum(pb0_b, own_b, PB0_B), column0, False)

    where = slot_index[0]
    at_slot = sub == where

    def new_products(q, acc):
        for u in range(8):
            j = q * 8 + u
            off = pl.ds(pl.multiple_of(j * LANES, LANES), LANES)
            fresh = jnp.broadcast_to(rnew[pl.ds(j, 1), :], (8, LANES))
            kept = jnp.where(at_slot, fresh, res[:, off])
            res[:, off] = kept
            rho[:, off] = jnp.where(at_slot, jnp.broadcast_to(den[pl.ds(j, 1), :], (8, LANES)), rho[:, off])
            acc = acc + kept * (fresh * jnp.broadcast_to(w[pl.ds(j, 1), :], (8, LANES)))
        return acc

    acc = lax.fori_loop(0, blocks // 8, new_products, zero)
    total = jnp.sum(acc, axis=1, keepdims=True)
    int1_a[own_a] = sublane_total(jnp.where(lane == sub, total, 0.0))[0:1, :]
    gather(int1_a, own_a, INT1_A, peers_a)
    int1_b[own_b] = group_sum(int1_a, own_a, INT1_A)
    gather(int1_b, own_b, INT1_B, peers_b)
    row = group_sum(int1_b, own_b, INT1_B)
    entries[40:48, :] = entry_values(row, 8)
    fresh_row = [splat(40, i) for i in range(HIST)]
    column1 = history_column(
        mixing_weights([
            [jnp.where(where == i, fresh_row[j], jnp.where(where == j, fresh_row[i], pair(i, j))) for j in range(i + 1)]
            for i in range(HIST)
        ])
    )

    put_moments(pb1_a, own_a, *batch_moments(column1))
    gather(pb1_a, own_a, PB1_A, peers_a)
    arrived(pb1_a, PB1_A, GROUP - 1)
    sides = left_sides(pb1_a)
    contributions(sides, same_atom, send1)
    scatter(send1, pb1_b, PB1_B)
    contributions(sides, same_slot, send2)
    scatter(send2, mom_b, MOM_B)
    mixed_total = group_sum(pb1_b, own_b, PB1_B)
    owned = group_sum(mom_b, own_b, MOM_B) * moment_scale
    mom_z[me["z"]] = owned
    for dz in range(1, 8):
        send(mom_z.at[me["z"]], mom_z.at[me["z"]], MOM_Z, {"z": lax.rem(me["z"] + dz, 8)})
    mixed_density(mixed_total, column1, True)
    store_den = pltpu.make_async_copy(den, den_h, local_sem.at[ST_DEN])
    store_den.start()
    arrived(mom_z, MOM_Z, 7)
    low_half = iota((8, LANES), 1) < batches
    for q in range(4):
        first, second = mom_z[2 * q], mom_z[2 * q + 1]
        cols = slice(q * LANES, (q + 1) * LANES)
        is_low = iota((ROWS, LANES), 1) < batches
        low = jnp.where(is_low, first, pltpu.roll(second, batches, 1))
        high = jnp.where(is_low, pltpu.roll(first, batches, 1), second)
        mom[0:8, cols] = low[0:8]
        mom[8:16, cols] = high[0:8]
        mom[16:20, cols] = low[8:12]
        mom[20:24, cols] = high[8:12]
        mom[24:25, cols] = low[12:13]
    store_mom = pltpu.make_async_copy(mom, mom_h, local_sem.at[ST_MOM])
    store_mom.start()

    for buf, key, count in (
        (int0_a, INT0_A, 15), (int0_b, INT0_B, 15), (meta_a, META_A, 15), (meta_b, META_B, 15),
        (pb0_a, PB0_A, 15), (pb0_b, PB0_B, 15), (int1_a, INT1_A, 15), (int1_b, INT1_B, 15),
        (pb1_a, PB1_A, 15), (pb1_b, PB1_B, 15), (mom_b, MOM_B, 15), (mom_z, MOM_Z, 7),
    ):
        sent(buf, key, count)
    store_den.wait()
    store_mom.wait()


def local(weights, target, coupling, basis, rho_hist, res_hist, batch_atom, owner_slot, slot_index):
    points = weights.shape[0]
    blocks = points // LANES
    harmonics = basis.shape[0]
    batches = batch_atom.shape[0]
    slots = owner_slot.shape[0]
    dense = lambda x: x.reshape(blocks, LANES)
    atom_row = jnp.pad(batch_atom, (0, LANES - batches)).reshape(1, LANES)
    hbm = pl.BlockSpec(memory_space=pltpu.HBM)
    smem = pl.BlockSpec(memory_space=pltpu.SMEM)
    small = lambda: pltpu.VMEM((GROUP, 1, LANES), F32)
    block = lambda count: pltpu.VMEM((count, ROWS, LANES), F32)
    relation = pltpu.VMEM((GROUP * batches, GROUP * batches), jnp.bfloat16)
    density, moments = pl.pallas_call(
        body,
        out_shape=(
            jax.ShapeDtypeStruct((blocks, LANES), F32),
            jax.ShapeDtypeStruct((harmonics, slots // 8), F32),
        ),
        in_specs=[hbm] * 8 + [smem],
        out_specs=(hbm, hbm),
        scratch_shapes=[
            pltpu.VMEM((blocks, LANES), F32),
            pltpu.VMEM((blocks, LANES), F32),
            pltpu.VMEM((blocks, LANES), F32),
            pltpu.VMEM((harmonics, points), F32),
            pltpu.VMEM((HIST, points), F32),
            pltpu.VMEM((HIST, points), F32),
            pltpu.VMEM((1, LANES), jnp.int32),
            pltpu.VMEM((slots // LANES, LANES), jnp.int32),
            pltpu.VMEM((blocks, LANES), F32),
            pltpu.VMEM((blocks, LANES), F32),
            pltpu.VMEM((harmonics, slots // 8), F32),
            pltpu.VMEM((48, LANES), F32),
            relation,
            relation,
            small(), small(), small(), small(),
            pltpu.VMEM((GROUP, 2, LANES), jnp.int32),
            pltpu.VMEM((GROUP, 2, LANES), jnp.int32),
            block(GROUP), block(GROUP), block(GROUP), block(GROUP), block(GROUP), block(8),
            block(GROUP), block(GROUP), block(GROUP),
            pltpu.SemaphoreType.DMA((LOCALS,)),
            pltpu.SemaphoreType.DMA((EXCHANGES,)),
            pltpu.SemaphoreType.DMA((EXCHANGES,)),
        ],
        compiler_params=pltpu.CompilerParams(collective_id=0, has_side_effects=True),
    )(
        dense(weights), dense(target), dense(coupling), basis, rho_hist, res_hist,
        atom_row, owner_slot.reshape(slots // LANES, LANES), slot_index,
    )
    return density.reshape(points), moments


def solution(mesh):
    torus = Mesh(mesh.devices.reshape(tuple(SIZES.values())), AXES)
    points = P(AXES)
    rows = P(None, AXES)
    return jax.shard_map(
        local,
        mesh=torus,
        in_specs=(points, points, points, rows, rows, rows, points, P(), P()),
        out_specs=(points, P(None, ("x", "c"))),
        check_vma=False,
    )
```

time: 351 us -> 69.2 us (0.20)
  blocking collectives: 194 us -> 0 us
  between operations: 93.7 us -> 0.64 us
  Pallas kernels: 0 us -> 64.3 us
  waiting for transfers between devices: 16.4 us -> 0 us
  other arithmetic: 13.6 us -> 0 us
  local copies, waits for them, and re-layouts: 16.2 us -> 4.11 us
  starting transfers between devices: 8.09 us -> 0 us
  matrix products: 7.31 us -> 0 us
    psum x12 -> x0, blocking collectives: 146 us -> none  [over_axes(): value = lax.psum(value, axis)]
    pallas_call x0 -> x1, Pallas kernels: none -> 64.3 us  [local(): pl.pallas_call(body, out_shape=(jax.ShapeDtypeStruct((blocks, LANES), F32...]
    all_gather x2 -> x0, blocking collectives: 48.4 us -> none  [moments_total(): all_moments = lax.all_gather(owned_moms, ATOM, axis=1, tiled=True)]
    all_to_all x2 -> x0, waiting for transfers between devices: 16.4 us -> none  [sent_and_summed(): lax.all_to_all(in_blocks(value, dim, peers), axis, 0, 0, tiled=True)]
    all_to_all x2 -> x0, starting transfers between devices: 8.09 us -> none  [sent_and_summed(): lax.all_to_all(in_blocks(value, dim, peers), axis, 0, 0, tiled=True)]
    dot_general x10 -> x0, matrix products: 7.31 us -> none  [the longest x2 1.47 us: local(): jnp.dot(all_moments * damping[:, None], one_hot.T, precision=hi_prec)]
    another operation x11 -> x0, other arithmetic: 6.35 us -> none
    reduce_sum x8 -> x0, other arithmetic: 5.22 us -> none  [the longest x2 2.01 us: local(): per_batch = jnp.sum(weighted * basis_blocks[None], axis=3)]
  transfers between devices with their start and end apart: 2 -> 0, of which waited for: 2 -> 0; matrix products, arithmetic and copies ran while one was open for 1% -> 0% of each run, Pallas kernels for 0% -> 0%
where the time goes in v1:
time: 69.2 us; the launch traced here: 69 us
  Pallas kernels  64.3 us (93%)
  local copies, waits for them, and re-layouts  4.11 us (6%)
    pallas_call x1, Pallas kernels, local(): pl.pallas_call(body, out_shape=(jax.ShapeDtypeStruct((blocks, LANES), F32...  64.3 us
    unnamed x2, local copies, waits for them, and re-layouts  2.95 us

profile of v1, /device:TPU:1, one launch (start us, length us, event | category | flops | bytes accessed | tf_op | source)
XLA Modules:
  0.0 69.0 jit_solution(16815286242603252032)
XLA Ops:
  0.6 1.2 %pad_bitcast_fusion.atom_h = s32[1,128]{1,0:T(1,128)} fusion(s32[64]{0:T(128)} %param.15), kind=kLoop, calls=%fused_computation | loop fusion | bytes 768 | tf_op jit(solution)/shard_map/reshape | solution.py:439
  1.8 64.3 %shard_map.104 = (f32[128,128]{1,0:T(8,128)}, f32[25,512]{1,0:T(8,128)}) custom-call(f32[128,128]{1,0:T(8,128)} %bitcast.7, f32[128,128]{1,0:T(8,128)} %bitcast.8, f32[128,128]{1,0:T(8,128)} %bitcast.9, f32[25,16384]{1,0:T(8,128)} %basis_h.1, f32[8,16384]{1,0:T(8,128)} %rho_h.1, f32[8,16384]{1,0:T(8,128)} %res_h.1, s32[1,128]{1,0:T(1,128)} %pad_bitcast_fusion.atom_h, ...), custom_call_target="tpu_custom_call" | custom-call | tf_op jit(solution)/shard_map/pallas_call | solution.py:445
  66.1 1.5 %copy.13 = f32[16384]{0:T(1024)} copy(f32[16384]{0:T(1024)} %bitcast.10) | data formatting | bytes 131072
  67.6 1.5 %copy.14 = f32[25,512]{1,0:T(8,128)} copy(f32[25,512]{1,0:T(8,128)} %get-tuple-element.9) | data formatting | bytes 102400

commit v2 on v1

--- a/solution.py
+++ b/solution.py
@@ -1,3 +1,5 @@
+import itertools
+
 import jax
 import jax.numpy as jnp
 from jax import lax
@@ -16,7 +18,7 @@
 RIDGE_SHARE = 0.1
 GROUP = 16
 ROWS = 13
-INT0_A, INT0_B, META_A, META_B, PB0_A, PB0_B, INT1_A, INT1_B, PB1_A, PB1_B, MOM_B, MOM_Z = range(12)
+INT0_A, INT0_B, ATOM_A, ATOM_B, SLOT_A, HIST_A, NEW_A, INT1_B, PB0_B, PB1_B, MOM_B, MOM_Z = range(12)
 EXCHANGES = 12
 LD_RES, LD_W, LD_ATOM, LD_OWNER, LD_BASIS, LD_RHO, LD_TARGET, LD_COUPLING, ST_DEN, ST_MOM = range(10)
 LOCALS = 10
@@ -83,10 +85,10 @@
 def body(
     w_h, t_h, cpl_h, basis_h, rho_h, res_h, atom_h, owner_h, slot_index,
     den_h, mom_h,
-    w, t, cpl, basis, rho, res, atom, owner, den, rnew, mom,
+    w, t, cpl, basis, rho, res, wres, atom, owner, den, rnew, mom,
     entries, same_atom, same_slot,
-    int0_a, int0_b, int1_a, int1_b, meta_a, meta_b,
-    pb0_a, pb0_b, pb1_a, pb1_b, mom_b, mom_z, send0, send1, send2,
+    int0_a, int0_b, int1_b, atom_a, atom_b, slot_a,
+    hist_a, new_a, pb0_b, pb1_b, mom_b, mom_z, send0, send1, send2,
     local_sem, send_sem, recv_sem,
 ):
     me = {name: lax.axis_index(name) for name in AXES}
@@ -102,16 +104,13 @@
         loads[key] = pltpu.make_async_copy(src, dst, local_sem.at[key])
         loads[key].start()
 
-    peers_a = []
-    for dy in range(4):
-        for dx in range(4):
-            if dy or dx:
-                peers_a.append({"y": lax.rem(me["y"] + dy, 4), "x": lax.rem(me["x"] + dx, 4)})
-    peers_b = []
-    for dc in range(2):
-        for dz in range(8):
-            if dc or dz:
-                peers_b.append({"z": lax.rem(me["z"] + dz, 8), "c": lax.rem(me["c"] + dc, 2)})
+    def peers(*names):
+        steps = [s for s in itertools.product(*(range(SIZES[name]) for name in names)) if any(s)]
+        hops = lambda s: sum(min(d, SIZES[name] - d) for d, name in zip(s, names))
+        steps.sort(key=hops, reverse=True)
+        return [{name: lax.rem(me[name] + d, SIZES[name]) for d, name in zip(s, names)} for s in steps]
+
+    peers_a, peers_b, peers_z = peers("y", "x"), peers("z", "c"), peers("z")
 
     barrier = pltpu.get_barrier_semaphore()
     for peer in peers_a + peers_b:
@@ -147,6 +146,7 @@
             off = pl.multiple_of((q * 8 + u) * LANES, LANES)
             r = res[:, pl.ds(off, LANES)]
             rw = r * jnp.broadcast_to(w[pl.ds(q * 8 + u, 1), :], (8, LANES))
+            wres[:, pl.ds(off, LANES)] = rw
             accs[0] = accs[0] + rw * r
             for s in range(1, 5):
                 accs[s] = accs[s] + rw * pltpu.roll(r, s, 0)
@@ -160,18 +160,58 @@
         placed = jnp.where(lane == 8 * s + sub, total, placed)
     int0_a[own_a] = sublane_total(placed)[0:1, :]
 
+    batches = 64
+    loads[LD_BASIS].wait()
+
+    def place(b, parts, k01, k2):
+        k01 = jnp.where(lane == b, parts[0], k01)
+        k01 = jnp.where(lane == b + batches, parts[1], k01)
+        return k01, jnp.where(lane == b + jnp.where(sub >= 4, batches, 0), parts[2], k2)
+
+    def history_batch(b, carry):
+        carry = list(carry)
+        offs = [pl.ds(pl.multiple_of((2 * b + h) * LANES, LANES), LANES) for h in range(2)]
+        tiles = [[basis[kt * 8:kt * 8 + 8, off] for off in offs] for kt in range(3)]
+        for i in range(HIST):
+            field = [jnp.broadcast_to(wres[i:i + 1, off], (8, LANES)) for off in offs]
+            parts = [
+                jnp.sum(tiles[kt][0] * field[0] + tiles[kt][1] * field[1], axis=1, keepdims=True) for kt in range(3)
+            ]
+            carry[2 * i], carry[2 * i + 1] = place(b, parts, carry[2 * i], carry[2 * i + 1])
+        last = [wres[:, off] * jnp.broadcast_to(basis[24:25, off], (8, LANES)) for off in offs]
+        last = jnp.sum(last[0] + last[1], axis=1, keepdims=True)
+        carry[16] = jnp.where(lane == b, last, carry[16])
+        return tuple(carry)
+
+    def put_moments(buf, at, k01, k2, k3):
+        buf[(*at, slice(0, 8))] = k01
+        buf[(*at, slice(8, 12))] = (k2 + pltpu.roll(k2, 4, 0))[0:4]
+        buf[(*at, slice(12, 13))] = k3
+
+    moments0 = lax.fori_loop(0, batches, history_batch, (zero,) * 17, unroll=2)
+    for i in range(HIST):
+        put_moments(hist_a, (own_a, i), moments0[2 * i], moments0[2 * i + 1], moments0[16][i:i + 1])
+
+    loads[LD_ATOM].wait()
+    atom_wide = jnp.concatenate([atom[...], atom[...]], axis=1)
+    atom_a[own_a] = atom_wide
+    atom_b[own_b] = atom_wide
+
     pl.semaphore_wait(barrier, len(peers_a) + len(peers_b))
     gather(int0_a, own_a, INT0_A, peers_a)
-
-    loads[LD_ATOM].wait()
+    gather(atom_a, own_a, ATOM_A, peers_a)
+    gather(atom_b, own_b, ATOM_B, peers_b)
+    gather(hist_a, own_a, HIST_A, peers_a)
+
     loads[LD_OWNER].wait()
-    batches = 64
     wide_sub = iota((batches, LANES), 0)
     wide_lane = iota((batches, LANES), 1)
-    atom_row = atom[0:1, :].astype(F32)
-    atom_col = jnp.sum(
-        jnp.where(wide_lane == wide_sub, jnp.broadcast_to(atom_row, (batches, LANES)), 0.0), axis=1, keepdims=True
-    )
+    own_lane = wide_lane == wide_sub
+
+    def as_column(row):
+        return jnp.sum(jnp.where(own_lane, jnp.broadcast_to(row, (batches, LANES)), 0.0), axis=1, keepdims=True)
+
+    atom_col = as_column(atom_wide.astype(F32))
 
     def look_up(j, found):
         owners = jnp.broadcast_to(owner[pl.ds(j, 1), :].astype(F32), (batches, LANES))
@@ -180,17 +220,8 @@
 
     found = lax.fori_loop(0, owner.shape[0], look_up, jnp.zeros((batches, LANES), F32))
     slot_col = jnp.sum(found, axis=1, keepdims=True)
-    slot_wide = jnp.sum(
-        jnp.where((wide_lane == wide_sub) | (wide_lane == wide_sub + batches), slot_col, 0.0), axis=0, keepdims=True
-    )
-    atom_wide = jnp.sum(
-        jnp.where((wide_lane == wide_sub) | (wide_lane == wide_sub + batches), atom_col, 0.0), axis=0, keepdims=True
-    )
-    meta = jnp.concatenate([atom_wide, slot_wide], axis=0).astype(jnp.int32)
-    meta_a[own_a] = meta
-    meta_b[own_b] = meta
-    gather(meta_a, own_a, META_A, peers_a)
-    gather(meta_b, own_b, META_B, peers_b)
+    slot_a[own_a] = jnp.sum(jnp.where(own_lane, slot_col, 0.0), axis=0, keepdims=True).astype(jnp.int32)
+    gather(slot_a, own_a, SLOT_A, peers_a)
 
     def group_sum(buf, own, key):
         arrived(buf, key, GROUP - 1)
@@ -202,19 +233,16 @@
     int0_b[own_b] = group_sum(int0_a, own_a, INT0_A)
     gather(int0_b, own_b, INT0_B, peers_b)
 
-    arrived(meta_a, META_A, GROUP - 1)
-    arrived(meta_b, META_B, GROUP - 1)
+    arrived(atom_a, ATOM_A, GROUP - 1)
+    arrived(atom_b, ATOM_B, GROUP - 1)
+    arrived(slot_a, SLOT_A, GROUP - 1)
     half = iota((1, LANES), 1) < batches
-    atoms_b = [
-        jnp.where(half, meta_b[2 * q, 0:1, :], meta_b[2 * q + 1, 0:1, :]).astype(F32) for q in range(GROUP // 2)
-    ]
+    atoms_b = [jnp.where(half, atom_b[2 * q], atom_b[2 * q + 1]).astype(F32) for q in range(GROUP // 2)]
     slot_base = me["x"] * (GROUP * batches)
 
     def relate(s, nothing):
-        both = meta_a[s].astype(F32)
-        own_lane = wide_lane == wide_sub
-        atoms_a = jnp.sum(jnp.where(own_lane, jnp.broadcast_to(both[0:1], (batches, LANES)), 0.0), axis=1, keepdims=True)
-        slots_a = jnp.sum(jnp.where(own_lane, jnp.broadcast_to(both[1:2], (batches, LANES)), 0.0), axis=1, keepdims=True)
+        atoms_a = as_column(atom_a[s].astype(F32))
+        slots_a = as_column(slot_a[s].astype(F32))
         at = pl.ds(pl.multiple_of(s * batches, batches), batches)
         for q in range(GROUP // 2):
             cols = pl.ds(q * LANES, LANES)
@@ -234,43 +262,11 @@
     def splat(base, i):
         return jnp.broadcast_to(entries[pl.ds(base + i, 1), :], (8, LANES))
 
-    def batch_moments(column):
-        def four(q, carry):
-            k01, k2, k3 = carry
-            for u in range(4):
-                b = q * 4 + u
-                offs, field = [], []
-                for h in range(2):
-                    j = q * 8 + 2 * u + h
-                    off = pl.ds(pl.multiple_of(j * LANES, LANES), LANES)
-                    mixed = sublane_total(column * res[:, off])
-                    field.append(mixed * jnp.broadcast_to(w[pl.ds(j, 1), :], (8, LANES)))
-                    offs.append(off)
-                parts = []
-                for kt in range(3):
-                    rows = pl.ds(kt * 8, 8)
-                    product = basis[rows, offs[0]] * field[0] + basis[rows, offs[1]] * field[1]
-                    parts.append(jnp.sum(product, axis=1, keepdims=True))
-                last = basis[24:25, offs[0]] * field[0][0:1] + basis[24:25, offs[1]] * field[1][0:1]
-                last = jnp.sum(last, axis=1, keepdims=True)
-                k01 = jnp.where(lane == b, parts[0], k01)
-                k01 = jnp.where(lane == b + batches, parts[1], k01)
-                k2 = jnp.where(lane == b + jnp.where(sub >= 4, batches, 0), parts[2], k2)
-                k3 = jnp.where(lane[0:1] == b, last, k3)
-            return k01, k2, k3
-
-        return lax.fori_loop(0, batches // 4, four, (zero, zero, zero[0:1]))
-
-    def put_moments(buf, at, k01, k2, k3):
-        buf[at, 0:8] = k01
-        buf[at, 8:12] = (k2 + pltpu.roll(k2, 4, 0))[0:4]
-        buf[at, 12:13] = k3
-
-    def left_sides(buf):
+    def left_sides(block_of):
         is_low = iota((ROWS, LANES), 1) < batches
         lows, highs = [], []
         for q in range(GROUP // 2):
-            first, second = buf[2 * q], buf[2 * q + 1]
+            first, second = block_of(2 * q), block_of(2 * q + 1)
             lows.append(jnp.where(is_low, first, pltpu.roll(second, batches, 1)))
             highs.append(jnp.where(is_low, pltpu.roll(first, batches, 1), second))
         pad = jnp.zeros((16 - ROWS, GROUP * batches), F32)
@@ -345,12 +341,17 @@
         s = (i - j) % 8
         return splat(0, 8 * s + i) if s <= 4 else splat(0, 8 * ((j - i) % 8) + j)
 
-    column0 = history_column(mixing_weights([[pair(i, j) for j in range(i + 1)] for i in range(HIST)]))
-    loads[LD_BASIS].wait()
-    put_moments(pb0_a, own_a, *batch_moments(column0))
-    gather(pb0_a, own_a, PB0_A, peers_a)
-    arrived(pb0_a, PB0_A, GROUP - 1)
-    contributions(left_sides(pb0_a), same_atom, send0)
+    weights0 = mixing_weights([[pair(i, j) for j in range(i + 1)] for i in range(HIST)])
+    column0 = history_column(weights0)
+
+    def mixed_block(values, s):
+        total = jnp.broadcast_to(values[0][0:1], (ROWS, LANES)) * hist_a[s, 0]
+        for i in range(1, HIST):
+            total = total + jnp.broadcast_to(values[i][0:1], (ROWS, LANES)) * hist_a[s, i]
+        return total
+
+    arrived(hist_a, HIST_A, GROUP - 1)
+    contributions(left_sides(lambda s: mixed_block(weights0, s)), same_atom, send0)
     scatter(send0, pb0_b, PB0_B)
     loads[LD_RHO].wait()
     loads[LD_TARGET].wait()
@@ -360,37 +361,63 @@
     where = slot_index[0]
     at_slot = sub == where
 
-    def new_products(q, acc):
+    def new_batches(q, carry):
+        acc, k01, k2, k3 = carry
+        for u in range(4):
+            b = q * 4 + u
+            offs = [pl.ds(pl.multiple_of((2 * b + h) * LANES, LANES), LANES) for h in range(2)]
+            field = []
+            for h in range(2):
+                fresh = jnp.broadcast_to(rnew[pl.ds(2 * b + h, 1), :], (8, LANES))
+                field.append(fresh * jnp.broadcast_to(w[pl.ds(2 * b + h, 1), :], (8, LANES)))
+                acc = acc + jnp.where(at_slot, fresh, res[:, offs[h]]) * field[h]
+            parts = []
+            for kt in range(3):
+                rows = slice(kt * 8, kt * 8 + 8)
+                product = basis[rows, offs[0]] * field[0] + basis[rows, offs[1]] * field[1]
+                parts.append(jnp.sum(product, axis=1, keepdims=True))
+            last = basis[24:25, offs[0]] * field[0][0:1] + basis[24:25, offs[1]] * field[1][0:1]
+            k01, k2 = place(b, parts, k01, k2)
+            k3 = jnp.where(lane[0:1] == b, jnp.sum(last, axis=1, keepdims=True), k3)
+        return acc, k01, k2, k3
+
+    acc, k01, k2, k3 = lax.fori_loop(0, batches // 4, new_batches, (zero, zero, zero, zero[0:1]))
+    total = jnp.sum(acc, axis=1, keepdims=True)
+    row = sublane_total(jnp.where(lane == sub + batches, total, 0.0))[0:1, :]
+    put_moments(new_a, (own_a,), k01, k2, jnp.where(half, k3, row))
+    gather(new_a, own_a, NEW_A, peers_a)
+
+    def overwrite(q, nothing):
         for u in range(8):
             j = q * 8 + u
             off = pl.ds(pl.multiple_of(j * LANES, LANES), LANES)
-            fresh = jnp.broadcast_to(rnew[pl.ds(j, 1), :], (8, LANES))
-            kept = jnp.where(at_slot, fresh, res[:, off])
-            res[:, off] = kept
+            res[:, off] = jnp.where(at_slot, jnp.broadcast_to(rnew[pl.ds(j, 1), :], (8, LANES)), res[:, off])
             rho[:, off] = jnp.where(at_slot, jnp.broadcast_to(den[pl.ds(j, 1), :], (8, LANES)), rho[:, off])
-            acc = acc + kept * (fresh * jnp.broadcast_to(w[pl.ds(j, 1), :], (8, LANES)))
-        return acc
-
-    acc = lax.fori_loop(0, blocks // 8, new_products, zero)
-    total = jnp.sum(acc, axis=1, keepdims=True)
-    int1_a[own_a] = sublane_total(jnp.where(lane == sub, total, 0.0))[0:1, :]
-    gather(int1_a, own_a, INT1_A, peers_a)
-    int1_b[own_b] = group_sum(int1_a, own_a, INT1_A)
+        return nothing
+
+    lax.fori_loop(0, blocks // 8, overwrite, 0)
+    arrived(new_a, NEW_A, GROUP - 1)
+    row = new_a[0, 12:13]
+    for s in range(1, GROUP):
+        row = row + new_a[s, 12:13]
+    int1_b[own_b] = pltpu.roll(row, batches, 1)
     gather(int1_b, own_b, INT1_B, peers_b)
     row = group_sum(int1_b, own_b, INT1_B)
     entries[40:48, :] = entry_values(row, 8)
     fresh_row = [splat(40, i) for i in range(HIST)]
-    column1 = history_column(
-        mixing_weights([
-            [jnp.where(where == i, fresh_row[j], jnp.where(where == j, fresh_row[i], pair(i, j))) for j in range(i + 1)]
-            for i in range(HIST)
-        ])
+    weights1 = mixing_weights([
+        [jnp.where(where == i, fresh_row[j], jnp.where(where == j, fresh_row[i], pair(i, j))) for j in range(i + 1)]
+        for i in range(HIST)
+    ])
+    column1 = history_column(weights1)
+
+    kept = [jnp.where(where == i, 0.0, weights1[i]) for i in range(HIST)]
+    fresh_weight = jnp.where(where == 0, weights1[0], 0.0)
+    for i in range(1, HIST):
+        fresh_weight = fresh_weight + jnp.where(where == i, weights1[i], 0.0)
+    sides = left_sides(
+        lambda s: mixed_block(kept, s) + jnp.broadcast_to(fresh_weight[0:1], (ROWS, LANES)) * new_a[s]
     )
-
-    put_moments(pb1_a, own_a, *batch_moments(column1))
-    gather(pb1_a, own_a, PB1_A, peers_a)
-    arrived(pb1_a, PB1_A, GROUP - 1)
-    sides = left_sides(pb1_a)
     contributions(sides, same_atom, send1)
     scatter(send1, pb1_b, PB1_B)
     contributions(sides, same_slot, send2)
@@ -398,13 +425,11 @@
     mixed_total = group_sum(pb1_b, own_b, PB1_B)
     owned = group_sum(mom_b, own_b, MOM_B) * moment_scale
     mom_z[me["z"]] = owned
-    for dz in range(1, 8):
-        send(mom_z.at[me["z"]], mom_z.at[me["z"]], MOM_Z, {"z": lax.rem(me["z"] + dz, 8)})
+    gather(mom_z, me["z"], MOM_Z, peers_z)
     mixed_density(mixed_total, column1, True)
     store_den = pltpu.make_async_copy(den, den_h, local_sem.at[ST_DEN])
     store_den.start()
     arrived(mom_z, MOM_Z, 7)
-    low_half = iota((8, LANES), 1) < batches
     for q in range(4):
         first, second = mom_z[2 * q], mom_z[2 * q + 1]
         cols = slice(q * LANES, (q + 1) * LANES)
@@ -420,9 +445,9 @@
     store_mom.start()
 
     for buf, key, count in (
-        (int0_a, INT0_A, 15), (int0_b, INT0_B, 15), (meta_a, META_A, 15), (meta_b, META_B, 15),
-        (pb0_a, PB0_A, 15), (pb0_b, PB0_B, 15), (int1_a, INT1_A, 15), (int1_b, INT1_B, 15),
-        (pb1_a, PB1_A, 15), (pb1_b, PB1_B, 15), (mom_b, MOM_B, 15), (mom_z, MOM_Z, 7),
+        (int0_a, INT0_A, 15), (int0_b, INT0_B, 15), (atom_a, ATOM_A, 15), (atom_b, ATOM_B, 15),
+        (slot_a, SLOT_A, 15), (hist_a, HIST_A, 15), (new_a, NEW_A, 15), (int1_b, INT1_B, 15),
+        (pb0_b, PB0_B, 15), (pb1_b, PB1_B, 15), (mom_b, MOM_B, 15), (mom_z, MOM_Z, 7),
     ):
         sent(buf, key, count)
     store_den.wait()
@@ -436,10 +461,9 @@
     batches = batch_atom.shape[0]
     slots = owner_slot.shape[0]
     dense = lambda x: x.reshape(blocks, LANES)
-    atom_row = jnp.pad(batch_atom, (0, LANES - batches)).reshape(1, LANES)
     hbm = pl.BlockSpec(memory_space=pltpu.HBM)
     smem = pl.BlockSpec(memory_space=pltpu.SMEM)
-    small = lambda: pltpu.VMEM((GROUP, 1, LANES), F32)
+    small = lambda dtype: pltpu.VMEM((GROUP, 1, LANES), dtype)
     block = lambda count: pltpu.VMEM((count, ROWS, LANES), F32)
     relation = pltpu.VMEM((GROUP * batches, GROUP * batches), jnp.bfloat16)
     density, moments = pl.pallas_call(
@@ -457,7 +481,8 @@
             pltpu.VMEM((harmonics, points), F32),
             pltpu.VMEM((HIST, points), F32),
             pltpu.VMEM((HIST, points), F32),
-            pltpu.VMEM((1, LANES), jnp.int32),
+            pltpu.VMEM((HIST, points), F32),
+            pltpu.VMEM((1, batches), jnp.int32),
             pltpu.VMEM((slots // LANES, LANES), jnp.int32),
             pltpu.VMEM((blocks, LANES), F32),
             pltpu.VMEM((blocks, LANES), F32),
@@ -465,10 +490,9 @@
             pltpu.VMEM((48, LANES), F32),
             relation,
             relation,
-            small(), small(), small(), small(),
-            pltpu.VMEM((GROUP, 2, LANES), jnp.int32),
-            pltpu.VMEM((GROUP, 2, LANES), jnp.int32),
-            block(GROUP), block(GROUP), block(GROUP), block(GROUP), block(GROUP), block(8),
+            small(F32), small(F32), small(F32), small(jnp.int32), small(jnp.int32), small(jnp.int32),
+            pltpu.VMEM((GROUP, HIST, ROWS, LANES), F32),
+            block(GROUP), block(GROUP), block(GROUP), block(GROUP), block(8),
             block(GROUP), block(GROUP), block(GROUP),
             pltpu.SemaphoreType.DMA((LOCALS,)),
             pltpu.SemaphoreType.DMA((EXCHANGES,)),
@@ -477,7 +501,7 @@
         compiler_params=pltpu.CompilerParams(collective_id=0, has_side_effects=True),
     )(
         dense(weights), dense(target), dense(coupling), basis, rho_hist, res_hist,
-        atom_row, owner_slot.reshape(slots // LANES, LANES), slot_index,
+        batch_atom.reshape(1, batches), owner_slot.reshape(slots // LANES, LANES), slot_index,
     )
     return density.reshape(points), moments
 

time: 69.2 us -> 63.3 us (0.915)
  Pallas kernels: 64.3 us -> 59.6 us
  local copies, waits for them, and re-layouts: 4.11 us -> 2.95 us
    pallas_call x1, Pallas kernels: 64.3 us -> 59.6 us  [local(): pl.pallas_call(body, out_shape=(jax.ShapeDtypeStruct((blocks, LANES), F32...]
    reshape x1 -> x0, local copies, waits for them, and re-layouts: 1.17 us -> none  [local(): atom_row = jnp.pad(batch_atom, (0, LANES - batches)).reshape(1, LANES)]
where the time goes in v2:
time: 63.3 us; the launch traced here: 63.1 us
  Pallas kernels  59.6 us (94%)
  local copies, waits for them, and re-layouts  2.95 us (5%)
  between operations  0.64 us (1%)
    pallas_call x1, Pallas kernels, local(): pl.pallas_call(body, out_shape=(jax.ShapeDtypeStruct((blocks, LANES), F32...  59.6 us
    unnamed x2, local copies, waits for them, and re-layouts  2.95 us

profile of v2, /device:TPU:1, one launch (start us, length us, event | category | flops | bytes accessed | tf_op | source)
XLA Modules:
  0.0 63.1 jit_solution(10909779450090828073)
XLA Ops:
  0.6 59.6 %shard_map.104 = (f32[128,128]{1,0:T(8,128)}, f32[25,512]{1,0:T(8,128)}) custom-call(f32[128,128]{1,0:T(8,128)} %bitcast.6, f32[128,128]{1,0:T(8,128)} %bitcast.7, f32[128,128]{1,0:T(8,128)} %bitcast.8, f32[25,16384]{1,0:T(8,128)} %basis_h.1, f32[8,16384]{1,0:T(8,128)} %rho_h.1, f32[8,16384]{1,0:T(8,128)} %res_h.1, s32[1,64]{1,0:T(1,128)} %bitcast.11, ...), custom_call_target="tpu_custom_call" | custom-call | tf_op jit(solution)/shard_map/pallas_call | solution.py:469
  60.2 1.5 %copy.13 = f32[16384]{0:T(1024)} copy(f32[16384]{0:T(1024)} %bitcast.9) | data formatting | bytes 131072
  61.7 1.5 %copy.14 = f32[25,512]{1,0:T(8,128)} copy(f32[25,512]{1,0:T(8,128)} %get-tuple-element.9) | data formatting | bytes 102400

commit v3 on v2

--- a/solution.py
+++ b/solution.py
@@ -18,10 +18,11 @@
 RIDGE_SHARE = 0.1
 GROUP = 16
 ROWS = 13
-INT0_A, INT0_B, ATOM_A, ATOM_B, SLOT_A, HIST_A, NEW_A, INT1_B, PB0_B, PB1_B, MOM_B, MOM_Z = range(12)
-EXCHANGES = 12
-LD_RES, LD_W, LD_ATOM, LD_OWNER, LD_BASIS, LD_RHO, LD_TARGET, LD_COUPLING, ST_DEN, ST_MOM = range(10)
-LOCALS = 10
+INT0_A, INT0_B, ATOM_A, ATOM_B, SLOT_A, HIST_0, HIST_1, HIST_2, HIST_3, NEW_A, INT1_B, PB0_B, PB1_B, MOM_B, MOM_Z = range(15)
+EXCHANGES = 15
+HIST_KEYS = (HIST_0, HIST_1, HIST_2, HIST_3)
+LD_RES, LD_W, LD_ATOM, LD_OWNER, LD_BASIS, LD_RHO, LD_TARGET, LD_COUPLING, LD_INDEX = range(9)
+LOCALS = 9
 
 
 def iota(shape, dim):
@@ -83,16 +84,17 @@
 
 
 def body(
-    w_h, t_h, cpl_h, basis_h, rho_h, res_h, atom_h, owner_h, slot_index,
-    den_h, mom_h,
-    w, t, cpl, basis, rho, res, wres, atom, owner, den, rnew, mom,
+    w_h, t_h, cpl_h, basis_h, rho_h, res_h, atom_h, owner_h, index_h,
+    den, mom,
+    w, t, cpl, basis, rho, res, wres, atom, owner, rnew, last_rows, slot_index,
     entries, same_atom, same_slot,
     int0_a, int0_b, int1_b, atom_a, atom_b, slot_a,
-    hist_a, new_a, pb0_b, pb1_b, mom_b, mom_z, send0, send1, send2,
+    hist_0, hist_1, hist_2, hist_3, new_a, pb0_b, pb1_b, mom_b, mom_z, send0, send1, send2,
     local_sem, send_sem, recv_sem,
 ):
     me = {name: lax.axis_index(name) for name in AXES}
     own_a = me["y"] * 4 + me["x"]
+    hist_a = (hist_0, hist_1, hist_2, hist_3)
     own_b = me["c"] * 8 + me["z"]
     blocks = w.shape[0]
 
@@ -100,6 +102,7 @@
     for key, src, dst in (
         (LD_RES, res_h, res), (LD_W, w_h, w), (LD_ATOM, atom_h, atom), (LD_OWNER, owner_h, owner),
         (LD_BASIS, basis_h, basis), (LD_RHO, rho_h, rho), (LD_TARGET, t_h, t), (LD_COUPLING, cpl_h, cpl),
+        (LD_INDEX, index_h, slot_index),
     ):
         loads[key] = pltpu.make_async_copy(src, dst, local_sem.at[key])
         loads[key].start()
@@ -168,40 +171,58 @@
         k01 = jnp.where(lane == b + batches, parts[1], k01)
         return k01, jnp.where(lane == b + jnp.where(sub >= 4, batches, 0), parts[2], k2)
 
-    def history_batch(b, carry):
-        carry = list(carry)
-        offs = [pl.ds(pl.multiple_of((2 * b + h) * LANES, LANES), LANES) for h in range(2)]
-        tiles = [[basis[kt * 8:kt * 8 + 8, off] for off in offs] for kt in range(3)]
-        for i in range(HIST):
-            field = [jnp.broadcast_to(wres[i:i + 1, off], (8, LANES)) for off in offs]
-            parts = [
-                jnp.sum(tiles[kt][0] * field[0] + tiles[kt][1] * field[1], axis=1, keepdims=True) for kt in range(3)
-            ]
-            carry[2 * i], carry[2 * i + 1] = place(b, parts, carry[2 * i], carry[2 * i + 1])
+    def batch_spans(b):
+        return [pl.ds(pl.multiple_of((2 * b + h) * LANES, LANES), LANES) for h in range(2)]
+
+    def chunk_moments(chunk):
+        def one(b, carry):
+            carry = list(carry)
+            offs = batch_spans(b)
+            tiles = [[basis[kt * 8:kt * 8 + 8, off] for off in offs] for kt in range(3)]
+            for n in range(2):
+                i = 2 * chunk + n
+                field = [jnp.broadcast_to(wres[i:i + 1, off], (8, LANES)) for off in offs]
+                parts = [
+                    jnp.sum(tiles[kt][0] * field[0] + tiles[kt][1] * field[1], axis=1, keepdims=True)
+                    for kt in range(3)
+                ]
+                carry[2 * n], carry[2 * n + 1] = place(b, parts, carry[2 * n], carry[2 * n + 1])
+            return tuple(carry)
+
+        return lax.fori_loop(0, batches, one, (zero,) * 4, unroll=8)
+
+    def last_harmonic(b, placed):
+        offs = batch_spans(b)
         last = [wres[:, off] * jnp.broadcast_to(basis[24:25, off], (8, LANES)) for off in offs]
-        last = jnp.sum(last[0] + last[1], axis=1, keepdims=True)
-        carry[16] = jnp.where(lane == b, last, carry[16])
-        return tuple(carry)
+        return jnp.where(lane == b, jnp.sum(last[0] + last[1], axis=1, keepdims=True), placed)
 
     def put_moments(buf, at, k01, k2, k3):
         buf[(*at, slice(0, 8))] = k01
         buf[(*at, slice(8, 12))] = (k2 + pltpu.roll(k2, 4, 0))[0:4]
         buf[(*at, slice(12, 13))] = k3
 
-    moments0 = lax.fori_loop(0, batches, history_batch, (zero,) * 17, unroll=2)
-    for i in range(HIST):
-        put_moments(hist_a, (own_a, i), moments0[2 * i], moments0[2 * i + 1], moments0[16][i:i + 1])
+    last_moments = lax.fori_loop(0, batches, last_harmonic, zero, unroll=8)
+
+    def fill_chunk(chunk):
+        found = chunk_moments(chunk)
+        for n in range(2):
+            i = 2 * chunk + n
+            put_moments(hist_a[chunk], (own_a, n), found[2 * n], found[2 * n + 1], last_moments[i:i + 1])
 
     loads[LD_ATOM].wait()
     atom_wide = jnp.concatenate([atom[...], atom[...]], axis=1)
     atom_a[own_a] = atom_wide
     atom_b[own_b] = atom_wide
+    fill_chunk(0)
 
     pl.semaphore_wait(barrier, len(peers_a) + len(peers_b))
     gather(int0_a, own_a, INT0_A, peers_a)
     gather(atom_a, own_a, ATOM_A, peers_a)
     gather(atom_b, own_b, ATOM_B, peers_b)
-    gather(hist_a, own_a, HIST_A, peers_a)
+    gather(hist_a[0], own_a, HIST_0, peers_a)
+    for chunk in range(1, 4):
+        fill_chunk(chunk)
+        gather(hist_a[chunk], own_a, HIST_KEYS[chunk], peers_a)
 
     loads[LD_OWNER].wait()
     wide_sub = iota((batches, LANES), 0)
@@ -235,23 +256,26 @@
 
     arrived(atom_a, ATOM_A, GROUP - 1)
     arrived(atom_b, ATOM_B, GROUP - 1)
-    arrived(slot_a, SLOT_A, GROUP - 1)
     half = iota((1, LANES), 1) < batches
     atoms_b = [jnp.where(half, atom_b[2 * q], atom_b[2 * q + 1]).astype(F32) for q in range(GROUP // 2)]
-    slot_base = me["x"] * (GROUP * batches)
-
-    def relate(s, nothing):
+
+    def relate_atoms(s, nothing):
         atoms_a = as_column(atom_a[s].astype(F32))
-        slots_a = as_column(slot_a[s].astype(F32))
         at = pl.ds(pl.multiple_of(s * batches, batches), batches)
         for q in range(GROUP // 2):
             cols = pl.ds(q * LANES, LANES)
             same_atom[at, cols] = jnp.where(atoms_a == atoms_b[q], 1.0, 0.0).astype(jnp.bfloat16)
-            number = (iota((1, LANES), 1) + (slot_base + q * LANES)).astype(F32)
-            same_slot[at, cols] = jnp.where(slots_a == number, 1.0, 0.0).astype(jnp.bfloat16)
         return nothing
 
-    lax.fori_loop(0, GROUP, relate, 0)
+    lax.fori_loop(0, GROUP, relate_atoms, 0)
+
+    def last_row(q, nothing):
+        for u in range(8):
+            j = q * 8 + u
+            last_rows[pl.ds(j, 1), :] = basis[24:25, pl.ds(pl.multiple_of(j * LANES, LANES), LANES)]
+        return nothing
+
+    lax.fori_loop(0, blocks // 8, last_row, 0)
 
     def entry_values(row, count):
         rows = iota((count, LANES), 0)
@@ -301,38 +325,59 @@
 
     moment_scale = 1.0 / 32.0
 
-    def mixed_density(total, column, final):
+    def folded(tiles):
+        for bit in (4, 2, 1):
+            low = (sub & bit) == 0
+            count = len(tiles) // 2
+            merged = []
+            for first, second in zip(tiles[:count], tiles[count:]):
+                given = jnp.where(low, second, first)
+                if bit == 4:
+                    given = pltpu.roll(given, 4, 0)
+                else:
+                    given = jnp.where(low, pltpu.roll(given, 8 - bit, 0), pltpu.roll(given, bit, 0))
+                merged.append(jnp.where(low, first, second) + given)
+            tiles = merged
+        return tiles[0]
+
+    def mix_history(column):
+        def eight(q, nothing):
+            offs = [pl.ds(pl.multiple_of((q * 8 + r) * LANES, LANES), LANES) for r in range(8)]
+            den[pl.ds(pl.multiple_of(q * 8, 8), 8), :] = folded(
+                [column * (rho[:, off] + MIX_BETA * res[:, off]) for off in offs]
+            )
+            return nothing
+
+        lax.fori_loop(0, blocks // 8, eight, 0, unroll=2)
+
+    def correct_density(total, final):
         total = total * (packed_scale(ROWS) * (MIX_BETA * moment_scale))
         first = total[0:8]
         rest = jnp.concatenate([total[8:13], jnp.zeros((3, LANES), F32)], axis=0)
         second = jnp.where(sub < 4, rest, pltpu.roll(pltpu.roll(rest, 4, 0), batches, 1))
         last = jnp.broadcast_to(rest[4:5], (8, LANES))
 
-        def eight(q, carry):
-            first, second, last = carry
-            dense = zero
+        def wide(x, b):
+            return jnp.broadcast_to(x[:, b:b + 1], (8, LANES))
+
+        for q in range(blocks // 8):
+            tiles = []
+            last_col = None
             for u in range(4):
-                cols = (
-                    jnp.broadcast_to(first[:, u:u + 1], (8, LANES)),
-                    jnp.broadcast_to(first[:, batches + u:batches + u + 1], (8, LANES)),
-                    jnp.broadcast_to(second[:, u:u + 1], (8, LANES)),
-                )
-                col_last = jnp.broadcast_to(last[:, u:u + 1], (8, LANES))
+                b = 4 * q + u
+                cols = (wide(first, b), wide(first, batches + b), wide(second, b))
+                col = wide(last, b)
+                last_col = col if u == 0 else jnp.where(sub >= 2 * u, col, last_col)
                 for h in range(2):
-                    r = 2 * u + h
-                    off = pl.ds(pl.multiple_of((q * 8 + r) * LANES, LANES), LANES)
-                    y = column * (rho[:, off] + MIX_BETA * res[:, off])
-                    for kt in range(3):
-                        y = y - cols[kt] * basis[kt * 8:kt * 8 + 8, off]
-                    y = sublane_total(y) - col_last * jnp.broadcast_to(basis[24:25, off], (8, LANES))
-                    dense = jnp.where(sub == r, y, dense)
-            at = pl.ds(pl.multiple_of(q * 8, 8), 8)
+                    off = slice((2 * b + h) * LANES, (2 * b + h + 1) * LANES)
+                    tiles.append(
+                        cols[0] * basis[0:8, off] + cols[1] * basis[8:16, off] + cols[2] * basis[16:24, off]
+                    )
+            at = slice(q * 8, q * 8 + 8)
+            dense = den[at, :] - folded(tiles) - last_col * last_rows[at, :]
             den[at, :] = dense
             if not final:
                 rnew[at, :] = t[at, :] + cpl[at, :] * jnp.tanh(dense) - dense
-            return tuple(pltpu.roll(x, LANES - 4, 1) for x in (first, second, last))
-
-        lax.fori_loop(0, blocks // 8, eight, (first, second, last))
 
     row = group_sum(int0_b, own_b, INT0_B)
     entries[0:40, :] = entry_values(row, 40)
@@ -345,18 +390,21 @@
     column0 = history_column(weights0)
 
     def mixed_block(values, s):
-        total = jnp.broadcast_to(values[0][0:1], (ROWS, LANES)) * hist_a[s, 0]
+        total = jnp.broadcast_to(values[0][0:1], (ROWS, LANES)) * hist_a[0][s, 0]
         for i in range(1, HIST):
-            total = total + jnp.broadcast_to(values[i][0:1], (ROWS, LANES)) * hist_a[s, i]
+            total = total + jnp.broadcast_to(values[i][0:1], (ROWS, LANES)) * hist_a[i // 2][s, i % 2]
         return total
 
-    arrived(hist_a, HIST_A, GROUP - 1)
+    for chunk in range(4):
+        arrived(hist_a[chunk], HIST_KEYS[chunk], GROUP - 1)
     contributions(left_sides(lambda s: mixed_block(weights0, s)), same_atom, send0)
     scatter(send0, pb0_b, PB0_B)
     loads[LD_RHO].wait()
     loads[LD_TARGET].wait()
     loads[LD_COUPLING].wait()
-    mixed_density(group_sum(pb0_b, own_b, PB0_B), column0, False)
+    loads[LD_INDEX].wait()
+    mix_history(column0)
+    correct_density(group_sum(pb0_b, own_b, PB0_B), False)
 
     where = slot_index[0]
     at_slot = sub == where
@@ -381,7 +429,7 @@
             k3 = jnp.where(lane[0:1] == b, jnp.sum(last, axis=1, keepdims=True), k3)
         return acc, k01, k2, k3
 
-    acc, k01, k2, k3 = lax.fori_loop(0, batches // 4, new_batches, (zero, zero, zero, zero[0:1]))
+    acc, k01, k2, k3 = lax.fori_loop(0, batches // 4, new_batches, (zero, zero, zero, zero[0:1]), unroll=4)
     total = jnp.sum(acc, axis=1, keepdims=True)
     row = sublane_total(jnp.where(lane == sub + batches, total, 0.0))[0:1, :]
     put_moments(new_a, (own_a,), k01, k2, jnp.where(half, k3, row))
@@ -396,6 +444,19 @@
         return nothing
 
     lax.fori_loop(0, blocks // 8, overwrite, 0)
+
+    arrived(slot_a, SLOT_A, GROUP - 1)
+    slot_base = me["x"] * (GROUP * batches)
+
+    def relate_slots(s, nothing):
+        slots_a = as_column(slot_a[s].astype(F32))
+        at = pl.ds(pl.multiple_of(s * batches, batches), batches)
+        for q in range(GROUP // 2):
+            number = (iota((1, LANES), 1) + (slot_base + q * LANES)).astype(F32)
+            same_slot[at, pl.ds(q * LANES, LANES)] = jnp.where(slots_a == number, 1.0, 0.0).astype(jnp.bfloat16)
+        return nothing
+
+    lax.fori_loop(0, GROUP, relate_slots, 0)
     arrived(new_a, NEW_A, GROUP - 1)
     row = new_a[0, 12:13]
     for s in range(1, GROUP):
@@ -422,13 +483,12 @@
     scatter(send1, pb1_b, PB1_B)
     contributions(sides, same_slot, send2)
     scatter(send2, mom_b, MOM_B)
+    mix_history(column1)
     mixed_total = group_sum(pb1_b, own_b, PB1_B)
     owned = group_sum(mom_b, own_b, MOM_B) * moment_scale
     mom_z[me["z"]] = owned
     gather(mom_z, me["z"], MOM_Z, peers_z)
-    mixed_density(mixed_total, column1, True)
-    store_den = pltpu.make_async_copy(den, den_h, local_sem.at[ST_DEN])
-    store_den.start()
+    correct_density(mixed_total, True)
     arrived(mom_z, MOM_Z, 7)
     for q in range(4):
         first, second = mom_z[2 * q], mom_z[2 * q + 1]
@@ -441,17 +501,22 @@
         mom[16:20, cols] = low[8:12]
         mom[20:24, cols] = high[8:12]
         mom[24:25, cols] = low[12:13]
-    store_mom = pltpu.make_async_copy(mom, mom_h, local_sem.at[ST_MOM])
-    store_mom.start()
 
     for buf, key, count in (
         (int0_a, INT0_A, 15), (int0_b, INT0_B, 15), (atom_a, ATOM_A, 15), (atom_b, ATOM_B, 15),
-        (slot_a, SLOT_A, 15), (hist_a, HIST_A, 15), (new_a, NEW_A, 15), (int1_b, INT1_B, 15),
+        (slot_a, SLOT_A, 15), (hist_0, HIST_0, 15), (hist_1, HIST_1, 15), (hist_2, HIST_2, 15), (hist_3, HIST_3, 15),
+        (new_a, NEW_A, 15), (int1_b, INT1_B, 15),
         (pb0_b, PB0_B, 15), (pb1_b, PB1_B, 15), (mom_b, MOM_B, 15), (mom_z, MOM_Z, 7),
     ):
         sent(buf, key, count)
-    store_den.wait()
-    store_mom.wait()
+
+
+def hand_over(den, mom, den_h, mom_h, sem):
+    copies = [pltpu.make_async_copy(den, den_h, sem.at[0]), pltpu.make_async_copy(mom, mom_h, sem.at[1])]
+    for copy in copies:
+        copy.start()
+    for copy in copies:
+        copy.wait()
 
 
 def local(weights, target, coupling, basis, rho_hist, res_hist, batch_atom, owner_slot, slot_index):
@@ -461,9 +526,14 @@
     batches = batch_atom.shape[0]
     slots = owner_slot.shape[0]
     dense = lambda x: x.reshape(blocks, LANES)
+    operands = (
+        dense(weights), dense(target), dense(coupling), basis, rho_hist, res_hist,
+        batch_atom.reshape(1, batches), owner_slot.reshape(slots // LANES, LANES), slot_index,
+    )
     hbm = pl.BlockSpec(memory_space=pltpu.HBM)
-    smem = pl.BlockSpec(memory_space=pltpu.SMEM)
+    vmem = pl.BlockSpec(memory_space=pltpu.VMEM)
     small = lambda dtype: pltpu.VMEM((GROUP, 1, LANES), dtype)
+    pair_block = lambda: pltpu.VMEM((GROUP, 2, ROWS, LANES), F32)
     block = lambda count: pltpu.VMEM((count, ROWS, LANES), F32)
     relation = pltpu.VMEM((GROUP * batches, GROUP * batches), jnp.bfloat16)
     density, moments = pl.pallas_call(
@@ -472,8 +542,8 @@
             jax.ShapeDtypeStruct((blocks, LANES), F32),
             jax.ShapeDtypeStruct((harmonics, slots // 8), F32),
         ),
-        in_specs=[hbm] * 8 + [smem],
-        out_specs=(hbm, hbm),
+        in_specs=[hbm] * len(operands),
+        out_specs=(vmem, vmem),
         scratch_shapes=[
             pltpu.VMEM((blocks, LANES), F32),
             pltpu.VMEM((blocks, LANES), F32),
@@ -486,23 +556,33 @@
             pltpu.VMEM((slots // LANES, LANES), jnp.int32),
             pltpu.VMEM((blocks, LANES), F32),
             pltpu.VMEM((blocks, LANES), F32),
-            pltpu.VMEM((harmonics, slots // 8), F32),
+            pltpu.SMEM((2,), jnp.int32),
             pltpu.VMEM((48, LANES), F32),
             relation,
             relation,
             small(F32), small(F32), small(F32), small(jnp.int32), small(jnp.int32), small(jnp.int32),
-            pltpu.VMEM((GROUP, HIST, ROWS, LANES), F32),
+            pair_block(), pair_block(), pair_block(), pair_block(),
             block(GROUP), block(GROUP), block(GROUP), block(GROUP), block(8),
             block(GROUP), block(GROUP), block(GROUP),
             pltpu.SemaphoreType.DMA((LOCALS,)),
             pltpu.SemaphoreType.DMA((EXCHANGES,)),
             pltpu.SemaphoreType.DMA((EXCHANGES,)),
         ],
-        compiler_params=pltpu.CompilerParams(collective_id=0, has_side_effects=True),
+        compiler_params=pltpu.CompilerParams(collective_id=0, has_side_effects=True, vmem_limit_bytes=24 << 20),
     )(
-        dense(weights), dense(target), dense(coupling), basis, rho_hist, res_hist,
-        batch_atom.reshape(1, batches), owner_slot.reshape(slots // LANES, LANES), slot_index,
+        *(pltpu.with_memory_space_constraint(x, pltpu.HBM) for x in operands)
     )
+    density, moments = pl.pallas_call(
+        hand_over,
+        out_shape=(
+            jax.ShapeDtypeStruct((blocks, LANES), F32),
+            jax.ShapeDtypeStruct((harmonics, slots // 8), F32),
+        ),
+        in_specs=[vmem, vmem],
+        out_specs=(hbm, hbm),
+        scratch_shapes=[pltpu.SemaphoreType.DMA((2,))],
+        compiler_params=pltpu.CompilerParams(vmem_limit_bytes=1 << 20),
+    )(density, moments)
     return density.reshape(points), moments
 
 

time: 63.3 us -> 52.2 us (0.82)
  Pallas kernels: 59.6 us -> 51.5 us
  local copies, waits for them, and re-layouts: 2.95 us -> 0 us
    pallas_call x1, Pallas kernels: 59.6 us -> 50.8 us  [local(): pl.pallas_call(body, out_shape=(jax.ShapeDtypeStruct((blocks, LANES), F32...]
    unnamed x2 -> x0, local copies, waits for them, and re-layouts: 2.95 us -> none
    pallas_call x0 -> x1, Pallas kernels: none -> 0.67 us  [local(): pl.pallas_call(hand_over, out_shape=(jax.ShapeDtypeStruct((blocks, LANES)...]
where the time goes in v3:
time: 52.2 us; the launch traced here: 52.1 us
  Pallas kernels  51.5 us (99%)
  between operations  0.64 us (1%)
    pallas_call x1, Pallas kernels, local(): pl.pallas_call(body, out_shape=(jax.ShapeDtypeStruct((blocks, LANES), F32...  50.8 us

profile of v3, /device:TPU:1, one launch (start us, length us, event | category | flops | bytes accessed | tf_op | source)
XLA Modules:
  0.0 52.1 jit_solution(2486177120125181433)
XLA Ops:
  0.6 50.8 %shard_map.104 = (f32[128,128]{1,0:T(8,128)S(1)}, f32[25,512]{1,0:T(8,128)S(1)}) custom-call(f32[128,128]{1,0:T(8,128)} %bitcast.6, f32[128,128]{1,0:T(8,128)} %bitcast.7, f32[128,128]{1,0:T(8,128)} %bitcast.8, f32[25,16384]{1,0:T(8,128)} %basis_h.1, f32[8,16384]{1,0:T(8,128)} %rho_h.1, f32[8,16384]{1,0:T(8,128)} %res_h.1, s32[1,64]{1,0:T(1,128)} %bitcast.10, ...), custom_call_target="tpu_custom_call" | custom-call | tf_op jit(solution)/shard_map/pallas_call | solution.py:539
  51.5 0.7 %shard_map.105 = (f32[128,128]{1,0:T(8,128)}, f32[25,512]{1,0:T(8,128)}) custom-call(f32[128,128]{1,0:T(8,128)S(1)} %get-tuple-element.6.den, f32[25,512]{1,0:T(8,128)S(1)} %get-tuple-element.7.mom), custom_call_target="tpu_custom_call" | custom-call | tf_op jit(solution)/shard_map/pallas_call | solution.py:575

commit v4 on v3

--- a/solution.py
+++ b/solution.py
@@ -18,8 +18,8 @@
 RIDGE_SHARE = 0.1
 GROUP = 16
 ROWS = 13
-INT0_A, INT0_B, ATOM_A, ATOM_B, SLOT_A, HIST_0, HIST_1, HIST_2, HIST_3, NEW_A, INT1_B, PB0_B, PB1_B, MOM_B, MOM_Z = range(15)
-EXCHANGES = 15
+INT0_A, INT0_B, ATOM_A, ATOM_B, SLOT_A, HIST_0, HIST_1, HIST_2, HIST_3, LAST_A, NEW_A, INT1_B, PB0_B, PB1_B, OLD_B, FRESH_B, MOM_ZY = range(17)
+EXCHANGES = 17
 HIST_KEYS = (HIST_0, HIST_1, HIST_2, HIST_3)
 LD_RES, LD_W, LD_ATOM, LD_OWNER, LD_BASIS, LD_RHO, LD_TARGET, LD_COUPLING, LD_INDEX = range(9)
 LOCALS = 9
@@ -87,9 +87,9 @@
     w_h, t_h, cpl_h, basis_h, rho_h, res_h, atom_h, owner_h, index_h,
     den, mom,
     w, t, cpl, basis, rho, res, wres, atom, owner, rnew, last_rows, slot_index,
-    entries, same_atom, same_slot,
+    entries, same_atom, owned_slot, sides8,
     int0_a, int0_b, int1_b, atom_a, atom_b, slot_a,
-    hist_0, hist_1, hist_2, hist_3, new_a, pb0_b, pb1_b, mom_b, mom_z, send0, send1, send2,
+    hist_0, hist_1, hist_2, hist_3, last_a, new_a, pb0_b, pb1_b, old_b, fresh_b, mom_zy, send0, send1, send_old, send_fresh,
     local_sem, send_sem, recv_sem,
 ):
     me = {name: lax.axis_index(name) for name in AXES}
@@ -113,7 +113,7 @@
         steps.sort(key=hops, reverse=True)
         return [{name: lax.rem(me[name] + d, SIZES[name]) for d, name in zip(s, names)} for s in steps]
 
-    peers_a, peers_b, peers_z = peers("y", "x"), peers("z", "c"), peers("z")
+    peers_a, peers_b, peers_zy = peers("y", "x"), peers("z", "c"), peers("z", "y")
 
     barrier = pltpu.get_barrier_semaphore()
     for peer in peers_a + peers_b:
@@ -196,18 +196,14 @@
         last = [wres[:, off] * jnp.broadcast_to(basis[24:25, off], (8, LANES)) for off in offs]
         return jnp.where(lane == b, jnp.sum(last[0] + last[1], axis=1, keepdims=True), placed)
 
-    def put_moments(buf, at, k01, k2, k3):
+    def put_moments(buf, at, k01, k2):
         buf[(*at, slice(0, 8))] = k01
         buf[(*at, slice(8, 12))] = (k2 + pltpu.roll(k2, 4, 0))[0:4]
-        buf[(*at, slice(12, 13))] = k3
-
-    last_moments = lax.fori_loop(0, batches, last_harmonic, zero, unroll=8)
 
     def fill_chunk(chunk):
         found = chunk_moments(chunk)
         for n in range(2):
-            i = 2 * chunk + n
-            put_moments(hist_a[chunk], (own_a, n), found[2 * n], found[2 * n + 1], last_moments[i:i + 1])
+            put_moments(hist_a[chunk], (own_a, n), found[2 * n], found[2 * n + 1])
 
     loads[LD_ATOM].wait()
     atom_wide = jnp.concatenate([atom[...], atom[...]], axis=1)
@@ -223,6 +219,8 @@
     for chunk in range(1, 4):
         fill_chunk(chunk)
         gather(hist_a[chunk], own_a, HIST_KEYS[chunk], peers_a)
+    last_a[own_a] = lax.fori_loop(0, batches, last_harmonic, zero, unroll=8)
+    gather(last_a, own_a, LAST_A, peers_a)
 
     loads[LD_OWNER].wait()
     wide_sub = iota((batches, LANES), 0)
@@ -389,22 +387,48 @@
     weights0 = mixing_weights([[pair(i, j) for j in range(i + 1)] for i in range(HIST)])
     column0 = history_column(weights0)
 
-    def mixed_block(values, s):
-        total = jnp.broadcast_to(values[0][0:1], (ROWS, LANES)) * hist_a[0][s, 0]
+    def history_block(i, s):
+        return jnp.concatenate([hist_a[i // 2][s, i % 2], last_a[s, i:i + 1]], axis=0)
+
+    def mixed_block(values, column, s):
+        total = jnp.broadcast_to(values[0][0:1], (ROWS - 1, LANES)) * hist_a[0][s, 0]
         for i in range(1, HIST):
-            total = total + jnp.broadcast_to(values[i][0:1], (ROWS, LANES)) * hist_a[i // 2][s, i % 2]
-        return total
+            total = total + jnp.broadcast_to(values[i][0:1], (ROWS - 1, LANES)) * hist_a[i // 2][s, i % 2]
+        return jnp.concatenate([total, sublane_total(column * last_a[s])[0:1]], axis=0)
 
     for chunk in range(4):
         arrived(hist_a[chunk], HIST_KEYS[chunk], GROUP - 1)
-    contributions(left_sides(lambda s: mixed_block(weights0, s)), same_atom, send0)
+    arrived(last_a, LAST_A, GROUP - 1)
+    contributions(left_sides(lambda s: mixed_block(weights0, column0, s)), same_atom, send0)
     scatter(send0, pb0_b, PB0_B)
     loads[LD_RHO].wait()
     loads[LD_TARGET].wait()
     loads[LD_COUPLING].wait()
     loads[LD_INDEX].wait()
     mix_history(column0)
-    correct_density(group_sum(pb0_b, own_b, PB0_B), False)
+
+    arrived(slot_a, SLOT_A, GROUP - 1)
+    place_of = iota((GROUP * 16, LANES), 0)
+    number = me["x"] * (GROUP * batches) + me["y"] * 4
+    number = number + (place_of >> 7) * 512 + ((place_of >> 4) & 7) * 16 + ((place_of >> 2) & 3) * LANES + (place_of & 3)
+    for q in range(GROUP // 2):
+        slots = jnp.where(half, slot_a[2 * q], pltpu.roll(slot_a[2 * q + 1], batches, 1))
+        owned_slot[:, q * LANES:(q + 1) * LANES] = jnp.where(number == slots, 1.0, 0.0).astype(jnp.bfloat16)
+
+    def slot_sums(parts):
+        return lax.dot_general(owned_slot[...], parts, (((1,), (1,)), ((), ())), preferred_element_type=F32)
+
+    for i in range(HIST):
+        parts = left_sides(lambda s: history_block(i, s))
+        for part in range(3):
+            sides8[part * 256 + i * 32:part * 256 + i * 32 + 32, :] = parts[part * 32:part * 32 + 32]
+    sums = slot_sums(sides8[...])
+    sums = sums[:, 0:256] + sums[:, 256:512] + sums[:, 512:768]
+    for p in range(GROUP):
+        send_old[p] = sums[p * 16:p * 16 + 16]
+    pb0_total = group_sum(pb0_b, own_b, PB0_B)
+    scatter(send_old, old_b, OLD_B)
+    correct_density(pb0_total, False)
 
     where = slot_index[0]
     at_slot = sub == where
@@ -432,7 +456,8 @@
     acc, k01, k2, k3 = lax.fori_loop(0, batches // 4, new_batches, (zero, zero, zero, zero[0:1]), unroll=4)
     total = jnp.sum(acc, axis=1, keepdims=True)
     row = sublane_total(jnp.where(lane == sub + batches, total, 0.0))[0:1, :]
-    put_moments(new_a, (own_a,), k01, k2, jnp.where(half, k3, row))
+    put_moments(new_a, (own_a,), k01, k2)
+    new_a[own_a, 12:13] = jnp.where(half, k3, row)
     gather(new_a, own_a, NEW_A, peers_a)
 
     def overwrite(q, nothing):
@@ -445,24 +470,18 @@
 
     lax.fori_loop(0, blocks // 8, overwrite, 0)
 
-    arrived(slot_a, SLOT_A, GROUP - 1)
-    slot_base = me["x"] * (GROUP * batches)
-
-    def relate_slots(s, nothing):
-        slots_a = as_column(slot_a[s].astype(F32))
-        at = pl.ds(pl.multiple_of(s * batches, batches), batches)
-        for q in range(GROUP // 2):
-            number = (iota((1, LANES), 1) + (slot_base + q * LANES)).astype(F32)
-            same_slot[at, pl.ds(q * LANES, LANES)] = jnp.where(slots_a == number, 1.0, 0.0).astype(jnp.bfloat16)
-        return nothing
-
-    lax.fori_loop(0, GROUP, relate_slots, 0)
     arrived(new_a, NEW_A, GROUP - 1)
     row = new_a[0, 12:13]
     for s in range(1, GROUP):
         row = row + new_a[s, 12:13]
     int1_b[own_b] = pltpu.roll(row, batches, 1)
     gather(int1_b, own_b, INT1_B, peers_b)
+    fresh_parts = left_sides(lambda s: new_a[s])
+    fresh_sums = slot_sums(jnp.concatenate([fresh_parts, jnp.zeros((32, GROUP * batches), jnp.bfloat16)], axis=0))
+    for p in range(GROUP):
+        send_fresh[p] = fresh_sums[p * 16:p * 16 + 16]
+    scatter(send_fresh, fresh_b, FRESH_B)
+    old_total = group_sum(old_b, own_b, OLD_B)
     row = group_sum(int1_b, own_b, INT1_B)
     entries[40:48, :] = entry_values(row, 8)
     fresh_row = [splat(40, i) for i in range(HIST)]
@@ -476,37 +495,54 @@
     fresh_weight = jnp.where(where == 0, weights1[0], 0.0)
     for i in range(1, HIST):
         fresh_weight = fresh_weight + jnp.where(where == i, weights1[i], 0.0)
+    kept_column = history_column(kept)
     sides = left_sides(
-        lambda s: mixed_block(kept, s) + jnp.broadcast_to(fresh_weight[0:1], (ROWS, LANES)) * new_a[s]
+        lambda s: mixed_block(kept, kept_column, s) + jnp.broadcast_to(fresh_weight[0:1], (ROWS, LANES)) * new_a[s]
     )
     contributions(sides, same_atom, send1)
     scatter(send1, pb1_b, PB1_B)
-    contributions(sides, same_slot, send2)
-    scatter(send2, mom_b, MOM_B)
+
+    part_of = lane >> 5
+    lower = kept[3]
+    upper = kept[7]
+    for n in range(3):
+        lower = jnp.where(part_of == n, kept[n], lower)
+        upper = jnp.where(part_of == n, kept[n + 4], upper)
+    fresh_total = group_sum(fresh_b, own_b, FRESH_B)
+    owned = []
+    for n in range(2):
+        rows = slice(8 * n, 8 * n + 8)
+        value = old_total[rows, 0:LANES] * lower + old_total[rows, LANES:2 * LANES] * upper
+        value = value + fresh_total[rows] * fresh_weight
+        value = value + pltpu.roll(value, 64, 1)
+        owned.append((value + pltpu.roll(value, 32, 1)) * moment_scale)
+    piece = jnp.where(
+        part_of < 2,
+        jnp.where(part_of == 0, owned[0], pltpu.roll(owned[0], 4, 0)),
+        jnp.where(part_of == 2, owned[1], pltpu.roll(owned[1], 4, 0)),
+    )
+    own_zy = me["z"] * 4 + me["y"]
+    mom_zy[own_zy] = piece[0:4]
+    gather(mom_zy, own_zy, MOM_ZY, peers_zy)
+
     mix_history(column1)
-    mixed_total = group_sum(pb1_b, own_b, PB1_B)
-    owned = group_sum(mom_b, own_b, MOM_B) * moment_scale
-    mom_z[me["z"]] = owned
-    gather(mom_z, me["z"], MOM_Z, peers_z)
-    correct_density(mixed_total, True)
-    arrived(mom_z, MOM_Z, 7)
-    for q in range(4):
-        first, second = mom_z[2 * q], mom_z[2 * q + 1]
-        cols = slice(q * LANES, (q + 1) * LANES)
-        is_low = iota((ROWS, LANES), 1) < batches
-        low = jnp.where(is_low, first, pltpu.roll(second, batches, 1))
-        high = jnp.where(is_low, pltpu.roll(first, batches, 1), second)
-        mom[0:8, cols] = low[0:8]
-        mom[8:16, cols] = high[0:8]
-        mom[16:20, cols] = low[8:12]
-        mom[20:24, cols] = high[8:12]
-        mom[24:25, cols] = low[12:13]
+    correct_density(group_sum(pb1_b, own_b, PB1_B), True)
+    arrived(mom_zy, MOM_ZY, len(peers_zy))
+    by_slot = jnp.concatenate([mom_zy[p] for p in range(32)], axis=0).T
+    for g in range(4):
+        cols, at = slice(g * LANES, (g + 1) * LANES), g * 32
+        mom[0:8, cols] = by_slot[at:at + 8]
+        mom[8:16, cols] = by_slot[at + 16:at + 24]
+        mom[16:20, cols] = by_slot[at + 8:at + 12]
+        mom[20:24, cols] = by_slot[at + 24:at + 28]
+        mom[24:25, cols] = by_slot[at + 12:at + 13]
 
     for buf, key, count in (
         (int0_a, INT0_A, 15), (int0_b, INT0_B, 15), (atom_a, ATOM_A, 15), (atom_b, ATOM_B, 15),
         (slot_a, SLOT_A, 15), (hist_0, HIST_0, 15), (hist_1, HIST_1, 15), (hist_2, HIST_2, 15), (hist_3, HIST_3, 15),
+        (last_a, LAST_A, 15),
         (new_a, NEW_A, 15), (int1_b, INT1_B, 15),
-        (pb0_b, PB0_B, 15), (pb1_b, PB1_B, 15), (mom_b, MOM_B, 15), (mom_z, MOM_Z, 7),
+        (pb0_b, PB0_B, 15), (pb1_b, PB1_B, 15), (old_b, OLD_B, 15), (fresh_b, FRESH_B, 15), (mom_zy, MOM_ZY, 31),
     ):
         sent(buf, key, count)
 
@@ -533,7 +569,7 @@
     hbm = pl.BlockSpec(memory_space=pltpu.HBM)
     vmem = pl.BlockSpec(memory_space=pltpu.VMEM)
     small = lambda dtype: pltpu.VMEM((GROUP, 1, LANES), dtype)
-    pair_block = lambda: pltpu.VMEM((GROUP, 2, ROWS, LANES), F32)
+    pair_block = lambda: pltpu.VMEM((GROUP, 2, ROWS - 1, LANES), F32)
     block = lambda count: pltpu.VMEM((count, ROWS, LANES), F32)
     relation = pltpu.VMEM((GROUP * batches, GROUP * batches), jnp.bfloat16)
     density, moments = pl.pallas_call(
@@ -559,11 +595,18 @@
             pltpu.SMEM((2,), jnp.int32),
             pltpu.VMEM((48, LANES), F32),
             relation,
-            relation,
+            pltpu.VMEM((GROUP * 16, GROUP * batches), jnp.bfloat16),
+            pltpu.VMEM((HIST * 3 * 32, GROUP * batches), jnp.bfloat16),
             small(F32), small(F32), small(F32), small(jnp.int32), small(jnp.int32), small(jnp.int32),
             pair_block(), pair_block(), pair_block(), pair_block(),
-            block(GROUP), block(GROUP), block(GROUP), block(GROUP), block(8),
+            pltpu.VMEM((GROUP, HIST, LANES), F32),
             block(GROUP), block(GROUP), block(GROUP),
+            pltpu.VMEM((GROUP, 16, 2 * LANES), F32),
+            pltpu.VMEM((GROUP, 16, LANES), F32),
+            pltpu.VMEM((32, 4, LANES), F32),
+            block(GROUP), block(GROUP),
+            pltpu.VMEM((GROUP, 16, 2 * LANES), F32),
+            pltpu.VMEM((GROUP, 16, LANES), F32),
             pltpu.SemaphoreType.DMA((LOCALS,)),
             pltpu.SemaphoreType.DMA((EXCHANGES,)),
             pltpu.SemaphoreType.DMA((EXCHANGES,)),

time: 52.2 us -> 48 us (0.920)
  Pallas kernels: 51.5 us -> 47.3 us
    pallas_call x1, Pallas kernels: 50.8 us -> 46.6 us  [local(): pl.pallas_call(body, out_shape=(jax.ShapeDtypeStruct((blocks, LANES), F32...]
where the time goes in v4:
time: 48 us; the launch traced here: 47.9 us
  Pallas kernels  47.3 us (99%)
  between operations  0.64 us (1%)
    pallas_call x1, Pallas kernels, local(): pl.pallas_call(body, out_shape=(jax.ShapeDtypeStruct((blocks, LANES), F32...  46.6 us

profile of v4, /device:TPU:1, one launch (start us, length us, event | category | flops | bytes accessed | tf_op | source)
XLA Modules:
  0.0 47.9 jit_solution(6693737325139338205)
XLA Ops:
  0.6 46.6 %shard_map.104 = (f32[128,128]{1,0:T(8,128)S(1)}, f32[25,512]{1,0:T(8,128)S(1)}) custom-call(f32[128,128]{1,0:T(8,128)} %bitcast.6, f32[128,128]{1,0:T(8,128)} %bitcast.7, f32[128,128]{1,0:T(8,128)} %bitcast.8, f32[25,16384]{1,0:T(8,128)} %basis_h.1, f32[8,16384]{1,0:T(8,128)} %rho_h.1, f32[8,16384]{1,0:T(8,128)} %res_h.1, s32[1,64]{1,0:T(1,128)} %bitcast.10, ...), custom_call_target="tpu_custom_call" | custom-call | tf_op jit(solution)/shard_map/pallas_call | solution.py:575
  47.3 0.7 %shard_map.105 = (f32[128,128]{1,0:T(8,128)}, f32[25,512]{1,0:T(8,128)}) custom-call(f32[128,128]{1,0:T(8,128)S(1)} %get-tuple-element.6.den, f32[25,512]{1,0:T(8,128)S(1)} %get-tuple-element.7.mom), custom_call_target="tpu_custom_call" | custom-call | tf_op jit(solution)/shard_map/pallas_call | solution.py:618

commit v5 on v4

--- a/solution.py
+++ b/solution.py
@@ -86,8 +86,8 @@
 def body(
     w_h, t_h, cpl_h, basis_h, rho_h, res_h, atom_h, owner_h, index_h,
     den, mom,
-    w, t, cpl, basis, rho, res, wres, atom, owner, rnew, last_rows, slot_index,
-    entries, same_atom, owned_slot, sides8,
+    w, t, cpl, basis, rho, res, wres, atom, owner, rnew, wnew, last_rows, slot_index,
+    entries, same_atom, owned_slot, sides8, old_out, fresh_out,
     int0_a, int0_b, int1_b, atom_a, atom_b, slot_a,
     hist_0, hist_1, hist_2, hist_3, last_a, new_a, pb0_b, pb1_b, old_b, fresh_b, mom_zy, send0, send1, send_old, send_fresh,
     local_sem, send_sem, recv_sem,
@@ -217,10 +217,13 @@
     gather(atom_b, own_b, ATOM_B, peers_b)
     gather(hist_a[0], own_a, HIST_0, peers_a)
     for chunk in range(1, 4):
+        if chunk == 3:
+            last = lax.fori_loop(0, batches, last_harmonic, zero, unroll=8)
+            last = jnp.where(lane < batches, last, pltpu.roll(pltpu.roll(last, 4, 0), batches, 1))
+            last_a[own_a] = last[0:4]
+            gather(last_a, own_a, LAST_A, peers_a)
         fill_chunk(chunk)
         gather(hist_a[chunk], own_a, HIST_KEYS[chunk], peers_a)
-    last_a[own_a] = lax.fori_loop(0, batches, last_harmonic, zero, unroll=8)
-    gather(last_a, own_a, LAST_A, peers_a)
 
     loads[LD_OWNER].wait()
     wide_sub = iota((batches, LANES), 0)
@@ -298,7 +301,9 @@
 
     def contributions(parts, matrix, out):
         result = jnp.dot(parts, matrix[...], preferred_element_type=F32)
-        result = result[0:32] + result[32:64] + result[64:96]
+        pack_contributions(result[0:32] + result[32:64] + result[64:96], out)
+
+    def pack_contributions(result, out):
         is_low = iota((ROWS, LANES), 1) < batches
         for q in range(GROUP // 2):
             cols = slice(q * LANES, (q + 1) * LANES)
@@ -375,7 +380,34 @@
             dense = den[at, :] - folded(tiles) - last_col * last_rows[at, :]
             den[at, :] = dense
             if not final:
-                rnew[at, :] = t[at, :] + cpl[at, :] * jnp.tanh(dense) - dense
+                fresh = t[at, :] + cpl[at, :] * jnp.tanh(dense) - dense
+                rnew[at, :] = fresh
+                wnew[at, :] = fresh * w[at, :]
+
+    def new_batches(at_slot):
+        def four(q, carry):
+            acc, k01, k2, k3 = carry
+            at = pl.ds(pl.multiple_of(q * 8, 8), 8)
+            found = jnp.sum(wnew[at, :] * last_rows[at, :], axis=1, keepdims=True)
+            k3 = jnp.where(lane == 4 * q + (sub >> 1), found, k3)
+            for u in range(4):
+                b = q * 4 + u
+                offs = batch_spans(b)
+                field = []
+                for h in range(2):
+                    field.append(jnp.broadcast_to(wnew[pl.ds(2 * b + h, 1), :], (8, LANES)))
+                    fresh = jnp.broadcast_to(rnew[pl.ds(2 * b + h, 1), :], (8, LANES))
+                    acc = acc + jnp.where(at_slot, fresh, res[:, offs[h]]) * field[h]
+                parts = []
+                for kt in range(3):
+                    rows = slice(kt * 8, kt * 8 + 8)
+                    product = basis[rows, offs[0]] * field[0] + basis[rows, offs[1]] * field[1]
+                    parts.append(jnp.sum(product, axis=1, keepdims=True))
+                k01, k2 = place(b, parts, k01, k2)
+            return acc, k01, k2, k3
+
+        acc, k01, k2, k3 = lax.fori_loop(0, batches // 4, four, (zero,) * 4, unroll=4)
+        return acc, k01, k2, sublane_total(k3)[0:1]
 
     row = group_sum(int0_b, own_b, INT0_B)
     entries[0:40, :] = entry_values(row, 40)
@@ -388,18 +420,22 @@
     column0 = history_column(weights0)
 
     def history_block(i, s):
-        return jnp.concatenate([hist_a[i // 2][s, i % 2], last_a[s, i:i + 1]], axis=0)
-
-    def mixed_block(values, column, s):
+        row = last_a[s, i % 4:i % 4 + 1]
+        return jnp.concatenate([hist_a[i // 2][s, i % 2], row if i < 4 else pltpu.roll(row, batches, 1)], axis=0)
+
+    def mixed_block(values, packed, s):
         total = jnp.broadcast_to(values[0][0:1], (ROWS - 1, LANES)) * hist_a[0][s, 0]
         for i in range(1, HIST):
             total = total + jnp.broadcast_to(values[i][0:1], (ROWS - 1, LANES)) * hist_a[i // 2][s, i % 2]
-        return jnp.concatenate([total, sublane_total(column * last_a[s])[0:1]], axis=0)
+        last = packed * last_a[s]
+        last = last[0:1] + last[1:2] + last[2:3] + last[3:4]
+        return jnp.concatenate([total, last + pltpu.roll(last, batches, 1)], axis=0)
 
     for chunk in range(4):
         arrived(hist_a[chunk], HIST_KEYS[chunk], GROUP - 1)
     arrived(last_a, LAST_A, GROUP - 1)
-    contributions(left_sides(lambda s: mixed_block(weights0, column0, s)), same_atom, send0)
+    packed0 = jnp.where(lane < batches, column0, pltpu.roll(column0, 4, 0))[0:4]
+    contributions(left_sides(lambda s: mixed_block(weights0, packed0, s)), same_atom, send0)
     scatter(send0, pb0_b, PB0_B)
     loads[LD_RHO].wait()
     loads[LD_TARGET].wait()
@@ -432,28 +468,7 @@
 
     where = slot_index[0]
     at_slot = sub == where
-
-    def new_batches(q, carry):
-        acc, k01, k2, k3 = carry
-        for u in range(4):
-            b = q * 4 + u
-            offs = [pl.ds(pl.multiple_of((2 * b + h) * LANES, LANES), LANES) for h in range(2)]
-            field = []
-            for h in range(2):
-                fresh = jnp.broadcast_to(rnew[pl.ds(2 * b + h, 1), :], (8, LANES))
-                field.append(fresh * jnp.broadcast_to(w[pl.ds(2 * b + h, 1), :], (8, LANES)))
-                acc = acc + jnp.where(at_slot, fresh, res[:, offs[h]]) * field[h]
-            parts = []
-            for kt in range(3):
-                rows = slice(kt * 8, kt * 8 + 8)
-                product = basis[rows, offs[0]] * field[0] + basis[rows, offs[1]] * field[1]
-                parts.append(jnp.sum(product, axis=1, keepdims=True))
-            last = basis[24:25, offs[0]] * field[0][0:1] + basis[24:25, offs[1]] * field[1][0:1]
-            k01, k2 = place(b, parts, k01, k2)
-            k3 = jnp.where(lane[0:1] == b, jnp.sum(last, axis=1, keepdims=True), k3)
-        return acc, k01, k2, k3
-
-    acc, k01, k2, k3 = lax.fori_loop(0, batches // 4, new_batches, (zero, zero, zero, zero[0:1]), unroll=4)
+    acc, k01, k2, k3 = new_batches(at_slot)
     total = jnp.sum(acc, axis=1, keepdims=True)
     row = sublane_total(jnp.where(lane == sub + batches, total, 0.0))[0:1, :]
     put_moments(new_a, (own_a,), k01, k2)
@@ -469,6 +484,10 @@
         return nothing
 
     lax.fori_loop(0, blocks // 8, overwrite, 0)
+    for n in range(4):
+        cols = slice(n * 256, n * 256 + 256)
+        out = jnp.dot(sides8[...], same_atom[:, cols], preferred_element_type=F32)
+        old_out[:, cols] = out[0:256] + out[256:512] + out[512:768]
 
     arrived(new_a, NEW_A, GROUP - 1)
     row = new_a[0, 12:13]
@@ -477,10 +496,27 @@
     int1_b[own_b] = pltpu.roll(row, batches, 1)
     gather(int1_b, own_b, INT1_B, peers_b)
     fresh_parts = left_sides(lambda s: new_a[s])
+    part_of = lane >> 5
+
+    def every_part(x):
+        x = x + pltpu.roll(x, 64, 1)
+        return x + pltpu.roll(x, 32, 1)
+
+    def packed_slots(low, high):
+        return jnp.where(
+            part_of < 2,
+            jnp.where(part_of == 0, low, pltpu.roll(low, 4, 0)),
+            jnp.where(part_of == 2, high, pltpu.roll(high, 4, 0)),
+        )[0:4]
+
     fresh_sums = slot_sums(jnp.concatenate([fresh_parts, jnp.zeros((32, GROUP * batches), jnp.bfloat16)], axis=0))
     for p in range(GROUP):
-        send_fresh[p] = fresh_sums[p * 16:p * 16 + 16]
+        send_fresh[p] = packed_slots(
+            every_part(fresh_sums[p * 16:p * 16 + 8]), every_part(fresh_sums[p * 16 + 8:p * 16 + 16])
+        )
     scatter(send_fresh, fresh_b, FRESH_B)
+    out = jnp.dot(fresh_parts, same_atom[...], preferred_element_type=F32)
+    fresh_out[...] = out[0:32] + out[32:64] + out[64:96]
     old_total = group_sum(old_b, own_b, OLD_B)
     row = group_sum(int1_b, own_b, INT1_B)
     entries[40:48, :] = entry_values(row, 8)
@@ -495,14 +531,21 @@
     fresh_weight = jnp.where(where == 0, weights1[0], 0.0)
     for i in range(1, HIST):
         fresh_weight = fresh_weight + jnp.where(where == i, weights1[i], 0.0)
-    kept_column = history_column(kept)
-    sides = left_sides(
-        lambda s: mixed_block(kept, kept_column, s) + jnp.broadcast_to(fresh_weight[0:1], (ROWS, LANES)) * new_a[s]
-    )
-    contributions(sides, same_atom, send1)
+    is_low = lane < batches
+    for q in range(GROUP // 2):
+        cols = slice(q * LANES, (q + 1) * LANES)
+        tiles = []
+        for r in range(4):
+            tile = fresh_weight * fresh_out[8 * r:8 * r + 8, cols]
+            for i in range(HIST):
+                tile = tile + kept[i] * old_out[i * 32 + 8 * r:i * 32 + 8 * r + 8, cols]
+            tiles.append(tile)
+        for low, high, rows in ((tiles[0], tiles[2], 8), (tiles[1], tiles[3], ROWS - 8)):
+            at = slice(0, 8) if rows == 8 else slice(8, ROWS)
+            send1[2 * q, at] = jnp.where(is_low, low, pltpu.roll(high, batches, 1))[0:rows]
+            send1[2 * q + 1, at] = jnp.where(is_low, pltpu.roll(low, batches, 1), high)[0:rows]
     scatter(send1, pb1_b, PB1_B)
 
-    part_of = lane >> 5
     lower = kept[3]
     upper = kept[7]
     for n in range(3):
@@ -513,16 +556,10 @@
     for n in range(2):
         rows = slice(8 * n, 8 * n + 8)
         value = old_total[rows, 0:LANES] * lower + old_total[rows, LANES:2 * LANES] * upper
-        value = value + fresh_total[rows] * fresh_weight
-        value = value + pltpu.roll(value, 64, 1)
-        owned.append((value + pltpu.roll(value, 32, 1)) * moment_scale)
-    piece = jnp.where(
-        part_of < 2,
-        jnp.where(part_of == 0, owned[0], pltpu.roll(owned[0], 4, 0)),
-        jnp.where(part_of == 2, owned[1], pltpu.roll(owned[1], 4, 0)),
-    )
+        owned.append(every_part(value))
+    piece = (packed_slots(*owned) + fresh_total * fresh_weight[0:4]) * moment_scale
     own_zy = me["z"] * 4 + me["y"]
-    mom_zy[own_zy] = piece[0:4]
+    mom_zy[own_zy] = piece
     gather(mom_zy, own_zy, MOM_ZY, peers_zy)
 
     mix_history(column1)
@@ -592,21 +629,24 @@
             pltpu.VMEM((slots // LANES, LANES), jnp.int32),
             pltpu.VMEM((blocks, LANES), F32),
             pltpu.VMEM((blocks, LANES), F32),
+            pltpu.VMEM((blocks, LANES), F32),
             pltpu.SMEM((2,), jnp.int32),
             pltpu.VMEM((48, LANES), F32),
             relation,
             pltpu.VMEM((GROUP * 16, GROUP * batches), jnp.bfloat16),
             pltpu.VMEM((HIST * 3 * 32, GROUP * batches), jnp.bfloat16),
+            pltpu.VMEM((HIST * 32, GROUP * batches), F32),
+            pltpu.VMEM((32, GROUP * batches), F32),
             small(F32), small(F32), small(F32), small(jnp.int32), small(jnp.int32), small(jnp.int32),
             pair_block(), pair_block(), pair_block(), pair_block(),
-            pltpu.VMEM((GROUP, HIST, LANES), F32),
+            pltpu.VMEM((GROUP, 4, LANES), F32),
             block(GROUP), block(GROUP), block(GROUP),
             pltpu.VMEM((GROUP, 16, 2 * LANES), F32),
-            pltpu.VMEM((GROUP, 16, LANES), F32),
+            pltpu.VMEM((GROUP, 4, LANES), F32),
             pltpu.VMEM((32, 4, LANES), F32),
             block(GROUP), block(GROUP),
             pltpu.VMEM((GROUP, 16, 2 * LANES), F32),
-            pltpu.VMEM((GROUP, 16, LANES), F32),
+            pltpu.VMEM((GROUP, 4, LANES), F32),
             pltpu.SemaphoreType.DMA((LOCALS,)),
             pltpu.SemaphoreType.DMA((EXCHANGES,)),
             pltpu.SemaphoreType.DMA((EXCHANGES,)),

time: 48 us -> 47.1 us (0.981)
  Pallas kernels: 47.3 us -> 46.2 us
    pallas_call x1, Pallas kernels: 46.6 us -> 45.6 us  [local(): pl.pallas_call(body, out_shape=(jax.ShapeDtypeStruct((blocks, LANES), F32...]
where the time goes in v5:
time: 47.1 us; the launch traced here: 46.9 us
  Pallas kernels  46.2 us (98%)
  between operations  0.64 us (1%)
    pallas_call x1, Pallas kernels, local(): pl.pallas_call(body, out_shape=(jax.ShapeDtypeStruct((blocks, LANES), F32...  45.6 us

profile of v5, /device:TPU:1, one launch (start us, length us, event | category | flops | bytes accessed | tf_op | source)
XLA Modules:
  0.0 46.9 jit_solution(4190356240999884119)
XLA Ops:
  0.6 45.6 %shard_map.104 = (f32[128,128]{1,0:T(8,128)S(1)}, f32[25,512]{1,0:T(8,128)S(1)}) custom-call(f32[128,128]{1,0:T(8,128)} %bitcast.6, f32[128,128]{1,0:T(8,128)} %bitcast.7, f32[128,128]{1,0:T(8,128)} %bitcast.8, f32[25,16384]{1,0:T(8,128)} %basis_h.1, f32[8,16384]{1,0:T(8,128)} %rho_h.1, f32[8,16384]{1,0:T(8,128)} %res_h.1, s32[1,64]{1,0:T(1,128)} %bitcast.10, ...), custom_call_target="tpu_custom_call" | custom-call | tf_op jit(solution)/shard_map/pallas_call | solution.py:612
  46.2 0.7 %shard_map.105 = (f32[128,128]{1,0:T(8,128)}, f32[25,512]{1,0:T(8,128)}) custom-call(f32[128,128]{1,0:T(8,128)S(1)} %get-tuple-element.6.den, f32[25,512]{1,0:T(8,128)S(1)} %get-tuple-element.7.mom), custom_call_target="tpu_custom_call" | custom-call | tf_op jit(solution)/shard_map/pallas_call | solution.py:658

commit v6 on v5

--- a/solution.py
+++ b/solution.py
@@ -18,8 +18,8 @@
 RIDGE_SHARE = 0.1
 GROUP = 16
 ROWS = 13
-INT0_A, INT0_B, ATOM_A, ATOM_B, SLOT_A, HIST_0, HIST_1, HIST_2, HIST_3, LAST_A, NEW_A, INT1_B, PB0_B, PB1_B, OLD_B, FRESH_B, MOM_ZY = range(17)
-EXCHANGES = 17
+INT0_A, INT0_B, ATOM_A, ATOM_B, SLOT_A, HIST_0, HIST_1, HIST_2, HIST_3, LAST_A, NEW_A, INT1_B, PB0_B, PB1_B, OLD_C, OLD_Z, FRESH_B, MOM_ZY = range(18)
+EXCHANGES = 18
 HIST_KEYS = (HIST_0, HIST_1, HIST_2, HIST_3)
 LD_RES, LD_W, LD_ATOM, LD_OWNER, LD_BASIS, LD_RHO, LD_TARGET, LD_COUPLING, LD_INDEX = range(9)
 LOCALS = 9
@@ -86,10 +86,10 @@
 def body(
     w_h, t_h, cpl_h, basis_h, rho_h, res_h, atom_h, owner_h, index_h,
     den, mom,
-    w, t, cpl, basis, rho, res, wres, atom, owner, rnew, wnew, last_rows, slot_index,
+    w, t, cpl, basis, rho, res, wres, atom, owner, rows8, mixed, w_t, target_t, coupling_t, mixed_t, den_t, fresh_t, basis_t, res_t, coef, slot_index,
     entries, same_atom, owned_slot, sides8, old_out, fresh_out,
     int0_a, int0_b, int1_b, atom_a, atom_b, slot_a,
-    hist_0, hist_1, hist_2, hist_3, last_a, new_a, pb0_b, pb1_b, old_b, fresh_b, mom_zy, send0, send1, send_old, send_fresh,
+    hist_0, hist_1, hist_2, hist_3, last_a, new_a, pb0_b, pb1_b, old_c, old_z, fresh_b, mom_zy, send0, send1, send_old, mine_old, send_fresh,
     local_sem, send_sem, recv_sem,
 ):
     me = {name: lax.axis_index(name) for name in AXES}
@@ -113,7 +113,7 @@
         steps.sort(key=hops, reverse=True)
         return [{name: lax.rem(me[name] + d, SIZES[name]) for d, name in zip(s, names)} for s in steps]
 
-    peers_a, peers_b, peers_zy = peers("y", "x"), peers("z", "c"), peers("z", "y")
+    peers_a, peers_b, peers_z, peers_zy = peers("y", "x"), peers("z", "c"), peers("z"), peers("z", "y")
 
     barrier = pltpu.get_barrier_semaphore()
     for peer in peers_a + peers_b:
@@ -245,14 +245,14 @@
     slot_a[own_a] = jnp.sum(jnp.where(own_lane, slot_col, 0.0), axis=0, keepdims=True).astype(jnp.int32)
     gather(slot_a, own_a, SLOT_A, peers_a)
 
-    def group_sum(buf, own, key):
-        arrived(buf, key, GROUP - 1)
+    def group_sum(buf, key, count=GROUP):
+        arrived(buf, key, count - 1)
         total = buf[0]
-        for i in range(1, GROUP):
+        for i in range(1, count):
             total = total + buf[i]
         return total
 
-    int0_b[own_b] = group_sum(int0_a, own_a, INT0_A)
+    int0_b[own_b] = group_sum(int0_a, INT0_A)
     gather(int0_b, own_b, INT0_B, peers_b)
 
     arrived(atom_a, ATOM_A, GROUP - 1)
@@ -270,13 +270,54 @@
 
     lax.fori_loop(0, GROUP, relate_atoms, 0)
 
+    def spread(tiles):
+        for bit in (4, 2, 1):
+            low = (sub & bit) == 0
+            swapped = list(tiles)
+            for j in range(8):
+                if not j & bit:
+                    first, second = tiles[j], tiles[j | bit]
+                    swapped[j] = jnp.where(low, first, pltpu.roll(second, bit, 0))
+                    swapped[j | bit] = jnp.where(low, pltpu.roll(first, 8 - bit, 0), second)
+            tiles = swapped
+        return tiles
+
+    def block_span(g, r):
+        j = 2 * (8 * (g & 7) + r) + (g >> 3)
+        return pl.ds(pl.multiple_of(j * LANES, LANES), LANES)
+
+    def group_rows(g):
+        return pl.ds(pl.multiple_of(g * 8, 8), 8)
+
+    def turn_rows(src, start, dst):
+        def collect(g, nothing):
+            for k, tile in enumerate(spread([src[start:start + 8, block_span(g, r)] for r in range(8)])):
+                rows8[k, group_rows(g), :] = tile
+            return nothing
+
+        lax.fori_loop(0, blocks // 8, collect, 0, unroll=2)
+
+        def turn(k, nothing):
+            dst[start + k] = rows8[k].T
+            return nothing
+
+        lax.fori_loop(0, 8, turn, 0, unroll=2)
+
+    def by_half(ref):
+        return jnp.concatenate([ref[pl.ds(0, blocks // 2, stride=2), :], ref[pl.ds(1, blocks // 2, stride=2), :]], axis=0)
+
+    for start in range(0, 24, 8):
+        turn_rows(basis, start, basis_t)
+
     def last_row(q, nothing):
         for u in range(8):
-            j = q * 8 + u
-            last_rows[pl.ds(j, 1), :] = basis[24:25, pl.ds(pl.multiple_of(j * LANES, LANES), LANES)]
+            at = (u % 2) * (blocks // 2) + q * 4 + u // 2
+            mixed[pl.ds(at, 1), :] = basis[24:25, pl.ds(pl.multiple_of((q * 8 + u) * LANES, LANES), LANES)]
         return nothing
 
     lax.fori_loop(0, blocks // 8, last_row, 0)
+    basis_t[24] = mixed[...].T
+    w_t[...] = by_half(w).T
 
     def entry_values(row, count):
         rows = iota((count, LANES), 0)
@@ -344,72 +385,70 @@
         return tiles[0]
 
     def mix_history(column):
-        def eight(q, nothing):
-            offs = [pl.ds(pl.multiple_of((q * 8 + r) * LANES, LANES), LANES) for r in range(8)]
-            den[pl.ds(pl.multiple_of(q * 8, 8), 8), :] = folded(
-                [column * (rho[:, off] + MIX_BETA * res[:, off]) for off in offs]
-            )
+        def eight(g, nothing):
+            offs = [block_span(g, r) for r in range(8)]
+            mixed[group_rows(g), :] = folded([column * (rho[:, off] + MIX_BETA * res[:, off]) for off in offs])
             return nothing
 
         lax.fori_loop(0, blocks // 8, eight, 0, unroll=2)
-
-    def correct_density(total, final):
+        return mixed[...].T
+
+    whole_half = lane < batches
+
+    def correct_density(total):
         total = total * (packed_scale(ROWS) * (MIX_BETA * moment_scale))
         first = total[0:8]
+        turned = pltpu.roll(first, batches, 1)
         rest = jnp.concatenate([total[8:13], jnp.zeros((3, LANES), F32)], axis=0)
-        second = jnp.where(sub < 4, rest, pltpu.roll(pltpu.roll(rest, 4, 0), batches, 1))
-        last = jnp.broadcast_to(rest[4:5], (8, LANES))
-
-        def wide(x, b):
-            return jnp.broadcast_to(x[:, b:b + 1], (8, LANES))
-
-        for q in range(blocks // 8):
-            tiles = []
-            last_col = None
-            for u in range(4):
-                b = 4 * q + u
-                cols = (wide(first, b), wide(first, batches + b), wide(second, b))
-                col = wide(last, b)
-                last_col = col if u == 0 else jnp.where(sub >= 2 * u, col, last_col)
-                for h in range(2):
-                    off = slice((2 * b + h) * LANES, (2 * b + h + 1) * LANES)
-                    tiles.append(
-                        cols[0] * basis[0:8, off] + cols[1] * basis[8:16, off] + cols[2] * basis[16:24, off]
-                    )
-            at = slice(q * 8, q * 8 + 8)
-            dense = den[at, :] - folded(tiles) - last_col * last_rows[at, :]
-            den[at, :] = dense
-            if not final:
-                fresh = t[at, :] + cpl[at, :] * jnp.tanh(dense) - dense
-                rnew[at, :] = fresh
-                wnew[at, :] = fresh * w[at, :]
-
-    def new_batches(at_slot):
-        def four(q, carry):
-            acc, k01, k2, k3 = carry
-            at = pl.ds(pl.multiple_of(q * 8, 8), 8)
-            found = jnp.sum(wnew[at, :] * last_rows[at, :], axis=1, keepdims=True)
-            k3 = jnp.where(lane == 4 * q + (sub >> 1), found, k3)
-            for u in range(4):
-                b = q * 4 + u
-                offs = batch_spans(b)
-                field = []
-                for h in range(2):
-                    field.append(jnp.broadcast_to(wnew[pl.ds(2 * b + h, 1), :], (8, LANES)))
-                    fresh = jnp.broadcast_to(rnew[pl.ds(2 * b + h, 1), :], (8, LANES))
-                    acc = acc + jnp.where(at_slot, fresh, res[:, offs[h]]) * field[h]
-                parts = []
-                for kt in range(3):
-                    rows = slice(kt * 8, kt * 8 + 8)
-                    product = basis[rows, offs[0]] * field[0] + basis[rows, offs[1]] * field[1]
-                    parts.append(jnp.sum(product, axis=1, keepdims=True))
-                k01, k2 = place(b, parts, k01, k2)
-            return acc, k01, k2, k3
-
-        acc, k01, k2, k3 = lax.fori_loop(0, batches // 4, four, (zero,) * 4, unroll=4)
-        return acc, k01, k2, sublane_total(k3)[0:1]
-
-    row = group_sum(int0_b, own_b, INT0_B)
+        rest_turned = pltpu.roll(rest, batches, 1)
+        low = jnp.where(whole_half, rest, rest_turned)
+        high = jnp.where(whole_half, rest_turned, rest)
+        coef[0:8] = jnp.where(whole_half, first, turned)
+        coef[8:16] = jnp.where(whole_half, turned, first)
+        coef[16:24] = jnp.where(sub < 4, low, pltpu.roll(high, 4, 0))
+        coef[24:25] = low[4:5]
+        factors = [jnp.broadcast_to(coef[k:k + 1, :], (8, LANES)) for k in range(25)]
+        found = []
+        for v in range(blocks // 8):
+            rows = slice(8 * v, 8 * v + 8)
+            value = factors[0] * basis_t[0, rows]
+            for k in range(1, 25):
+                value = value + factors[k] * basis_t[k, rows]
+            found.append(mixed_t[rows] - value)
+            den_t[rows] = found[-1]
+        return found
+
+    def add_up(terms):
+        while len(terms) > 1:
+            terms = [sum(terms[n:n + 2][1:], terms[n]) for n in range(0, len(terms), 2)]
+        return terms[0]
+
+    def new_moments(dense, where):
+        spans = [slice(8 * v, 8 * v + 8) for v in range(blocks // 8)]
+        fresh, weighted = [], []
+        for rows, value in zip(spans, dense):
+            fresh.append(target_t[rows] + coupling_t[rows] * jnp.tanh(value) - value)
+            fresh_t[rows] = fresh[-1]
+            weighted.append(fresh[-1] * w_t[rows])
+
+        def both_halves(x):
+            return x + pltpu.roll(x, batches, 1)
+
+        sums = [add_up([x * basis_t[k, rows] for x, rows in zip(weighted, spans)]) for k in range(25)]
+        k0, k1, k2 = (both_halves(folded(sums[kt * 8:kt * 8 + 8])) for kt in range(3))
+        k3 = both_halves(sublane_total(sums[24]))[0:1]
+        itself = add_up([x * y for x, y in zip(weighted, fresh)])
+        sums = [
+            jnp.where(where == i, itself, add_up([x * res_t[i, rows] for x, rows in zip(weighted, spans)]))
+            for i in range(HIST)
+        ]
+        total = jnp.sum(folded(sums), axis=1, keepdims=True)
+        row = sublane_total(jnp.where(lane == sub + batches, total, 0.0))[0:1, :]
+        new_a[own_a, 0:8] = jnp.where(whole_half, k0, k1)
+        new_a[own_a, 8:12] = jnp.where(whole_half, k2, pltpu.roll(k2, 4, 0))[0:4]
+        new_a[own_a, 12:13] = jnp.where(half, k3, row)
+
+    row = group_sum(int0_b, INT0_B)
     entries[0:40, :] = entry_values(row, 40)
 
     def pair(i, j):
@@ -441,7 +480,10 @@
     loads[LD_TARGET].wait()
     loads[LD_COUPLING].wait()
     loads[LD_INDEX].wait()
-    mix_history(column0)
+    mixed_t[...] = mix_history(column0)
+    target_t[...] = by_half(t).T
+    coupling_t[...] = by_half(cpl).T
+    turn_rows(res, 0, res_t)
 
     arrived(slot_a, SLOT_A, GROUP - 1)
     place_of = iota((GROUP * 16, LANES), 0)
@@ -462,28 +504,21 @@
     sums = sums[:, 0:256] + sums[:, 256:512] + sums[:, 512:768]
     for p in range(GROUP):
         send_old[p] = sums[p * 16:p * 16 + 16]
-    pb0_total = group_sum(pb0_b, own_b, PB0_B)
-    scatter(send_old, old_b, OLD_B)
-    correct_density(pb0_total, False)
+    other = 1 - me["c"]
+    send(send_old.at[pl.ds(other * 8, 8)], old_c, OLD_C, {"c": other})
+    pb0_total = group_sum(pb0_b, PB0_B)
 
     where = slot_index[0]
-    at_slot = sub == where
-    acc, k01, k2, k3 = new_batches(at_slot)
-    total = jnp.sum(acc, axis=1, keepdims=True)
-    row = sublane_total(jnp.where(lane == sub + batches, total, 0.0))[0:1, :]
-    put_moments(new_a, (own_a,), k01, k2)
-    new_a[own_a, 12:13] = jnp.where(half, k3, row)
+    new_moments(correct_density(pb0_total), where)
     gather(new_a, own_a, NEW_A, peers_a)
 
-    def overwrite(q, nothing):
-        for u in range(8):
-            j = q * 8 + u
-            off = pl.ds(pl.multiple_of(j * LANES, LANES), LANES)
-            res[:, off] = jnp.where(at_slot, jnp.broadcast_to(rnew[pl.ds(j, 1), :], (8, LANES)), res[:, off])
-            rho[:, off] = jnp.where(at_slot, jnp.broadcast_to(den[pl.ds(j, 1), :], (8, LANES)), rho[:, off])
-        return nothing
-
-    lax.fori_loop(0, blocks // 8, overwrite, 0)
+    arrived(old_c, OLD_C, 8)
+    for z in range(8):
+        mine_old[z] = send_old[me["c"] * 8 + z] + old_c[z]
+    old_z[me["z"]] = mine_old[me["z"]]
+    for peer in peers_z:
+        send(mine_old.at[peer["z"]], old_z.at[me["z"]], OLD_Z, peer)
+
     for n in range(4):
         cols = slice(n * 256, n * 256 + 256)
         out = jnp.dot(sides8[...], same_atom[:, cols], preferred_element_type=F32)
@@ -517,15 +552,14 @@
     scatter(send_fresh, fresh_b, FRESH_B)
     out = jnp.dot(fresh_parts, same_atom[...], preferred_element_type=F32)
     fresh_out[...] = out[0:32] + out[32:64] + out[64:96]
-    old_total = group_sum(old_b, own_b, OLD_B)
-    row = group_sum(int1_b, own_b, INT1_B)
+    old_total = group_sum(old_z, OLD_Z, 8)
+    row = group_sum(int1_b, INT1_B)
     entries[40:48, :] = entry_values(row, 8)
     fresh_row = [splat(40, i) for i in range(HIST)]
     weights1 = mixing_weights([
         [jnp.where(where == i, fresh_row[j], jnp.where(where == j, fresh_row[i], pair(i, j))) for j in range(i + 1)]
         for i in range(HIST)
     ])
-    column1 = history_column(weights1)
 
     kept = [jnp.where(where == i, 0.0, weights1[i]) for i in range(HIST)]
     fresh_weight = jnp.where(where == 0, weights1[0], 0.0)
@@ -551,7 +585,7 @@
     for n in range(3):
         lower = jnp.where(part_of == n, kept[n], lower)
         upper = jnp.where(part_of == n, kept[n + 4], upper)
-    fresh_total = group_sum(fresh_b, own_b, FRESH_B)
+    fresh_total = group_sum(fresh_b, FRESH_B)
     owned = []
     for n in range(2):
         rows = slice(8 * n, 8 * n + 8)
@@ -562,8 +596,13 @@
     mom_zy[own_zy] = piece
     gather(mom_zy, own_zy, MOM_ZY, peers_zy)
 
-    mix_history(column1)
-    correct_density(group_sum(pb1_b, own_b, PB1_B), True)
+    mixed_t[...] = mix_history(history_column(kept)) + jnp.broadcast_to(fresh_weight[0:1], (blocks, LANES)) * (
+        den_t[...] + MIX_BETA * fresh_t[...]
+    )
+    correct_density(group_sum(pb1_b, PB1_B))
+    by_block = den_t[...].T
+    den[pl.ds(0, blocks // 2, stride=2), :] = by_block[0:blocks // 2]
+    den[pl.ds(1, blocks // 2, stride=2), :] = by_block[blocks // 2:blocks]
     arrived(mom_zy, MOM_ZY, len(peers_zy))
     by_slot = jnp.concatenate([mom_zy[p] for p in range(32)], axis=0).T
     for g in range(4):
@@ -579,7 +618,7 @@
         (slot_a, SLOT_A, 15), (hist_0, HIST_0, 15), (hist_1, HIST_1, 15), (hist_2, HIST_2, 15), (hist_3, HIST_3, 15),
         (last_a, LAST_A, 15),
         (new_a, NEW_A, 15), (int1_b, INT1_B, 15),
-        (pb0_b, PB0_B, 15), (pb1_b, PB1_B, 15), (old_b, OLD_B, 15), (fresh_b, FRESH_B, 15), (mom_zy, MOM_ZY, 31),
+        (pb0_b, PB0_B, 15), (pb1_b, PB1_B, 15), (old_c, OLD_C, 8), (old_z, OLD_Z, 7), (fresh_b, FRESH_B, 15), (mom_zy, MOM_ZY, 31),
     ):
         sent(buf, key, count)
 
@@ -605,6 +644,7 @@
     )
     hbm = pl.BlockSpec(memory_space=pltpu.HBM)
     vmem = pl.BlockSpec(memory_space=pltpu.VMEM)
+    dense_rows = lambda: pltpu.VMEM((blocks, LANES), F32)
     small = lambda dtype: pltpu.VMEM((GROUP, 1, LANES), dtype)
     pair_block = lambda: pltpu.VMEM((GROUP, 2, ROWS - 1, LANES), F32)
     block = lambda count: pltpu.VMEM((count, ROWS, LANES), F32)
@@ -627,9 +667,11 @@
             pltpu.VMEM((HIST, points), F32),
             pltpu.VMEM((1, batches), jnp.int32),
             pltpu.VMEM((slots // LANES, LANES), jnp.int32),
-            pltpu.VMEM((blocks, LANES), F32),
-            pltpu.VMEM((blocks, LANES), F32),
-            pltpu.VMEM((blocks, LANES), F32),
+            pltpu.VMEM((8, blocks, LANES), F32),
+            dense_rows(), dense_rows(), dense_rows(), dense_rows(), dense_rows(), dense_rows(), dense_rows(),
+            pltpu.VMEM((harmonics, blocks, LANES), F32),
+            pltpu.VMEM((HIST, blocks, LANES), F32),
+            pltpu.VMEM((32, LANES), F32),
             pltpu.SMEM((2,), jnp.int32),
             pltpu.VMEM((48, LANES), F32),
             relation,
@@ -641,11 +683,13 @@
             pair_block(), pair_block(), pair_block(), pair_block(),
             pltpu.VMEM((GROUP, 4, LANES), F32),
             block(GROUP), block(GROUP), block(GROUP),
-            pltpu.VMEM((GROUP, 16, 2 * LANES), F32),
+            pltpu.VMEM((8, 16, 2 * LANES), F32),
+            pltpu.VMEM((8, 16, 2 * LANES), F32),
             pltpu.VMEM((GROUP, 4, LANES), F32),
             pltpu.VMEM((32, 4, LANES), F32),
             block(GROUP), block(GROUP),
             pltpu.VMEM((GROUP, 16, 2 * LANES), F32),
+            pltpu.VMEM((8, 16, 2 * LANES), F32),
             pltpu.VMEM((GROUP, 4, LANES), F32),
             pltpu.SemaphoreType.DMA((LOCALS,)),
             pltpu.SemaphoreType.DMA((EXCHANGES,)),

time: 47.1 us -> 46.4 us (0.985)
  Pallas kernels: 46.2 us -> 45.5 us
    pallas_call x1, Pallas kernels: 45.6 us -> 44.8 us  [local(): pl.pallas_call(body, out_shape=(jax.ShapeDtypeStruct((blocks, LANES), F32...]
where the time goes in v6:
time: 46.4 us; the launch traced here: 46.1 us
  Pallas kernels  45.5 us (98%)
  between operations  0.64 us (1%)
    pallas_call x1, Pallas kernels, local(): pl.pallas_call(body, out_shape=(jax.ShapeDtypeStruct((blocks, LANES), F32...  44.8 us

profile of v6, /device:TPU:1, one launch (start us, length us, event | category | flops | bytes accessed | tf_op | source)
XLA Modules:
  0.0 46.1 jit_solution(5871886698124869514)
XLA Ops:
  0.6 44.8 %shard_map.104 = (f32[128,128]{1,0:T(8,128)S(1)}, f32[25,512]{1,0:T(8,128)S(1)}) custom-call(f32[128,128]{1,0:T(8,128)} %bitcast.6, f32[128,128]{1,0:T(8,128)} %bitcast.7, f32[128,128]{1,0:T(8,128)} %bitcast.8, f32[25,16384]{1,0:T(8,128)} %basis_h.1, f32[8,16384]{1,0:T(8,128)} %rho_h.1, f32[8,16384]{1,0:T(8,128)} %res_h.1, s32[1,64]{1,0:T(1,128)} %bitcast.10, ...), custom_call_target="tpu_custom_call" | custom-call | tf_op jit(solution)/shard_map/pallas_call | solution.py:652
  45.4 0.7 %shard_map.105 = (f32[128,128]{1,0:T(8,128)}, f32[25,512]{1,0:T(8,128)}) custom-call(f32[128,128]{1,0:T(8,128)S(1)} %get-tuple-element.6.den, f32[25,512]{1,0:T(8,128)S(1)} %get-tuple-element.7.mom), custom_call_target="tpu_custom_call" | custom-call | tf_op jit(solution)/shard_map/pallas_call | solution.py:702

commit v7 on v6

--- a/solution.py
+++ b/solution.py
@@ -18,8 +18,8 @@
 RIDGE_SHARE = 0.1
 GROUP = 16
 ROWS = 13
-INT0_A, INT0_B, ATOM_A, ATOM_B, SLOT_A, HIST_0, HIST_1, HIST_2, HIST_3, LAST_A, NEW_A, INT1_B, PB0_B, PB1_B, OLD_C, OLD_Z, FRESH_B, MOM_ZY = range(18)
-EXCHANGES = 18
+INT0_A, INT0_B, ATOM_A, ATOM_B, SLOT_A, HIST_0, HIST_1, HIST_2, HIST_3, LAST_A, NEW_A, INT1_B, PB0_B, PB1_B, OLD_C, OLD_Z, FRESH_B, MOM_ZY, ON_A = range(19)
+EXCHANGES = 19
 HIST_KEYS = (HIST_0, HIST_1, HIST_2, HIST_3)
 LD_RES, LD_W, LD_ATOM, LD_OWNER, LD_BASIS, LD_RHO, LD_TARGET, LD_COUPLING, LD_INDEX = range(9)
 LOCALS = 9
@@ -99,25 +99,34 @@
     blocks = w.shape[0]
 
     loads = {}
-    for key, src, dst in (
-        (LD_RES, res_h, res), (LD_W, w_h, w), (LD_ATOM, atom_h, atom), (LD_OWNER, owner_h, owner),
-        (LD_BASIS, basis_h, basis), (LD_RHO, rho_h, rho), (LD_TARGET, t_h, t), (LD_COUPLING, cpl_h, cpl),
-        (LD_INDEX, index_h, slot_index),
-    ):
-        loads[key] = pltpu.make_async_copy(src, dst, local_sem.at[key])
-        loads[key].start()
-
-    def peers(*names):
+
+    def load(*copies):
+        for key, src, dst in copies:
+            loads[key] = pltpu.make_async_copy(src, dst, local_sem.at[key])
+            loads[key].start()
+
+    load((LD_RES, res_h, res), (LD_W, w_h, w), (LD_BASIS, basis_h, basis), (LD_ATOM, atom_h, atom))
+
+    def steps_along(*names):
         steps = [s for s in itertools.product(*(range(SIZES[name]) for name in names)) if any(s)]
         hops = lambda s: sum(min(d, SIZES[name] - d) for d, name in zip(s, names))
-        steps.sort(key=hops, reverse=True)
-        return [{name: lax.rem(me[name] + d, SIZES[name]) for d, name in zip(s, names)} for s in steps]
+        return sorted(steps, key=hops, reverse=True)
+
+    def peers(*names):
+        return [
+            {name: lax.rem(me[name] + d, SIZES[name]) for d, name in zip(s, names)} for s in steps_along(*names)
+        ]
 
     peers_a, peers_b, peers_z, peers_zy = peers("y", "x"), peers("z", "c"), peers("z"), peers("z", "y")
+    peers_near = [peer for peer, step in zip(peers_a, steps_along("y", "x")) if step[1] != 2]
 
     barrier = pltpu.get_barrier_semaphore()
     for peer in peers_a + peers_b:
         pl.semaphore_signal(barrier, inc=1, device_id=peer, device_id_type=MESH)
+    load(
+        (LD_OWNER, owner_h, owner), (LD_RHO, rho_h, rho), (LD_TARGET, t_h, t), (LD_COUPLING, cpl_h, cpl),
+        (LD_INDEX, index_h, slot_index),
+    )
 
     def send(src, dst, key, peer):
         pltpu.make_async_remote_copy(
@@ -215,7 +224,7 @@
     gather(int0_a, own_a, INT0_A, peers_a)
     gather(atom_a, own_a, ATOM_A, peers_a)
     gather(atom_b, own_b, ATOM_B, peers_b)
-    gather(hist_a[0], own_a, HIST_0, peers_a)
+    gather(hist_a[0], own_a, HIST_0, peers_near)
     for chunk in range(1, 4):
         if chunk == 3:
             last = lax.fori_loop(0, batches, last_harmonic, zero, unroll=8)
@@ -254,6 +263,12 @@
 
     int0_b[own_b] = group_sum(int0_a, INT0_A)
     gather(int0_b, own_b, INT0_B, peers_b)
+
+    arrived(hist_0, HIST_0, len(peers_near))
+    for y in range(4):
+        for n, step in ((0, 1), (1, 3)):
+            block_at = hist_0.at[y * 4 + lax.rem(me["x"] + 4 - step, 4), n]
+            send(block_at, block_at, ON_A, {"x": lax.rem(me["x"] + step, 4)})
 
     arrived(atom_a, ATOM_A, GROUP - 1)
     arrived(atom_b, ATOM_B, GROUP - 1)
@@ -470,7 +485,8 @@
         last = last[0:1] + last[1:2] + last[2:3] + last[3:4]
         return jnp.concatenate([total, last + pltpu.roll(last, batches, 1)], axis=0)
 
-    for chunk in range(4):
+    arrived(hist_0, ON_A, 4)
+    for chunk in range(1, 4):
         arrived(hist_a[chunk], HIST_KEYS[chunk], GROUP - 1)
     arrived(last_a, LAST_A, GROUP - 1)
     packed0 = jnp.where(lane < batches, column0, pltpu.roll(column0, 4, 0))[0:4]
@@ -615,7 +631,7 @@
 
     for buf, key, count in (
         (int0_a, INT0_A, 15), (int0_b, INT0_B, 15), (atom_a, ATOM_A, 15), (atom_b, ATOM_B, 15),
-        (slot_a, SLOT_A, 15), (hist_0, HIST_0, 15), (hist_1, HIST_1, 15), (hist_2, HIST_2, 15), (hist_3, HIST_3, 15),
+        (slot_a, SLOT_A, 15), (hist_0, HIST_0, 11), (hist_0, ON_A, 4), (hist_1, HIST_1, 15), (hist_2, HIST_2, 15), (hist_3, HIST_3, 15),
         (last_a, LAST_A, 15),
         (new_a, NEW_A, 15), (int1_b, INT1_B, 15),
         (pb0_b, PB0_B, 15), (pb1_b, PB1_B, 15), (old_c, OLD_C, 8), (old_z, OLD_Z, 7), (fresh_b, FRESH_B, 15), (mom_zy, MOM_ZY, 31),

time: 46.4 us -> 46 us (level)
  no operation moved by 1% of the time
where the time goes in v7:
time: 46 us; the launch traced here: 45.9 us
  Pallas kernels  45.3 us (98%)
  between operations  0.64 us (1%)
    pallas_call x1, Pallas kernels, local(): pl.pallas_call(body, out_shape=(jax.ShapeDtypeStruct((blocks, LANES), F32...  44.6 us

profile of v7, /device:TPU:1, one launch (start us, length us, event | category | flops | bytes accessed | tf_op | source)
XLA Modules:
  0.0 45.9 jit_solution(3715384763988492100)
XLA Ops:
  0.6 44.6 %shard_map.104 = (f32[128,128]{1,0:T(8,128)S(1)}, f32[25,512]{1,0:T(8,128)S(1)}) custom-call(f32[128,128]{1,0:T(8,128)} %bitcast.6, f32[128,128]{1,0:T(8,128)} %bitcast.7, f32[128,128]{1,0:T(8,128)} %bitcast.8, f32[25,16384]{1,0:T(8,128)} %basis_h.1, f32[8,16384]{1,0:T(8,128)} %rho_h.1, f32[8,16384]{1,0:T(8,128)} %res_h.1, s32[1,64]{1,0:T(1,128)} %bitcast.10, ...), custom_call_target="tpu_custom_call" | custom-call | tf_op jit(solution)/shard_map/pallas_call | solution.py:668
  45.3 0.7 %shard_map.105 = (f32[128,128]{1,0:T(8,128)}, f32[25,512]{1,0:T(8,128)}) custom-call(f32[128,128]{1,0:T(8,128)S(1)} %get-tuple-element.6.den, f32[25,512]{1,0:T(8,128)S(1)} %get-tuple-element.7.mom), custom_call_target="tpu_custom_call" | custom-call | tf_op jit(solution)/shard_map/pallas_call | solution.py:718

commit v8 on v7

--- a/solution.py
+++ b/solution.py
@@ -348,8 +348,9 @@
         lows, highs = [], []
         for q in range(GROUP // 2):
             first, second = block_of(2 * q), block_of(2 * q + 1)
-            lows.append(jnp.where(is_low, first, pltpu.roll(second, batches, 1)))
-            highs.append(jnp.where(is_low, pltpu.roll(first, batches, 1), second))
+            crossed = pltpu.roll(jnp.where(is_low, second, first), batches, 1)
+            lows.append(jnp.where(is_low, first, crossed))
+            highs.append(jnp.where(is_low, crossed, second))
         pad = jnp.zeros((16 - ROWS, GROUP * batches), F32)
         low = jnp.concatenate(lows, axis=1)
         high = jnp.concatenate(highs, axis=1)
@@ -364,8 +365,9 @@
         for q in range(GROUP // 2):
             cols = slice(q * LANES, (q + 1) * LANES)
             low, high = result[0:ROWS, cols], result[16:16 + ROWS, cols]
-            out[2 * q] = jnp.where(is_low, low, pltpu.roll(high, batches, 1))
-            out[2 * q + 1] = jnp.where(is_low, pltpu.roll(low, batches, 1), high)
+            crossed = pltpu.roll(jnp.where(is_low, high, low), batches, 1)
+            out[2 * q] = jnp.where(is_low, low, crossed)
+            out[2 * q + 1] = jnp.where(is_low, crossed, high)
 
     def scatter(out, buf, key):
         buf[own_b] = out[own_b]
@@ -592,8 +594,9 @@
             tiles.append(tile)
         for low, high, rows in ((tiles[0], tiles[2], 8), (tiles[1], tiles[3], ROWS - 8)):
             at = slice(0, 8) if rows == 8 else slice(8, ROWS)
-            send1[2 * q, at] = jnp.where(is_low, low, pltpu.roll(high, batches, 1))[0:rows]
-            send1[2 * q + 1, at] = jnp.where(is_low, pltpu.roll(low, batches, 1), high)[0:rows]
+            crossed = pltpu.roll(jnp.where(is_low, high, low), batches, 1)
+            send1[2 * q, at] = jnp.where(is_low, low, crossed)[0:rows]
+            send1[2 * q + 1, at] = jnp.where(is_low, crossed, high)[0:rows]
     scatter(send1, pb1_b, PB1_B)
 
     lower = kept[3]

time: 46 us -> 46 us (level)
  no operation moved by 1% of the time
where the time goes in v8:
time: 46 us; the launch traced here: 45.9 us
  Pallas kernels  45.3 us (98%)
  between operations  0.64 us (1%)
    pallas_call x1, Pallas kernels, local(): pl.pallas_call(body, out_shape=(jax.ShapeDtypeStruct((blocks, LANES), F32...  44.6 us

profile of v8, /device:TPU:1, one launch (start us, length us, event | category | flops | bytes accessed | tf_op | source)
XLA Modules:
  0.0 45.9 jit_solution(4017547578835519971)
XLA Ops:
  0.6 44.6 %shard_map.104 = (f32[128,128]{1,0:T(8,128)S(1)}, f32[25,512]{1,0:T(8,128)S(1)}) custom-call(f32[128,128]{1,0:T(8,128)} %bitcast.6, f32[128,128]{1,0:T(8,128)} %bitcast.7, f32[128,128]{1,0:T(8,128)} %bitcast.8, f32[25,16384]{1,0:T(8,128)} %basis_h.1, f32[8,16384]{1,0:T(8,128)} %rho_h.1, f32[8,16384]{1,0:T(8,128)} %res_h.1, s32[1,64]{1,0:T(1,128)} %bitcast.10, ...), custom_call_target="tpu_custom_call" | custom-call | tf_op jit(solution)/shard_map/pallas_call | solution.py:671
  45.3 0.7 %shard_map.105 = (f32[128,128]{1,0:T(8,128)}, f32[25,512]{1,0:T(8,128)}) custom-call(f32[128,128]{1,0:T(8,128)S(1)} %get-tuple-element.6.den, f32[25,512]{1,0:T(8,128)S(1)} %get-tuple-element.7.mom), custom_call_target="tpu_custom_call" | custom-call | tf_op jit(solution)/shard_map/pallas_call | solution.py:721
